TPU v7x, 32 devices: a whole 2x2x4 slice. The times are simulated.
32 devices in a mesh: group: 2 (over x), row: 4 (over y, core), col: 4 (over z).
Axes of the slice: x: 2, y: 2, z: 4, core: 2. Of those that a mesh axis runs over, the one named last changes fastest.
Arguments:
- pair_repr: bfloat16 [128, 128, 128], P(('group', 'row'), 'col'), may hold values from -6 to 6
- pair_mask: int32 [128, 128], P(('group', 'row'), 'col'), may hold values 0 or 1
- chain_id: int32 [128], replicated, may hold values from 0 to 7, never falling along the last dimension, each value on 1 to 32 neighbouring positions
- tri_in_gain: float32 [128], replicated, may hold values from 0.5 to 1.5
- tri_proj: bfloat16 [128, 512], replicated, may hold values from -0.5 to 0.5
- tri_gate: bfloat16 [128, 128], replicated, may hold values from -0.5 to 0.5
- tri_out_gain: float32 [128], replicated, may hold values from 0.5 to 1.5
- tri_out: bfloat16 [128, 128], replicated, may hold values from -0.5 to 0.5
- bias_gain: float32 [128], replicated, may hold values from 0.5 to 1.5
- bias_weight: bfloat16 [128, 16], replicated, may hold values from -0.5 to 0.5
- chain_bias: float32 [16], replicated, may hold values from -2 to 2
- tokens: bfloat16 [24, 128, 768], P(('group', 'row')), may hold values from -6 to 6
- noise_level: int32 [24], P(('group', 'row')), may hold values from 0 to 199
- attn_gain: float32 [768], replicated, may hold values from 0.5 to 1.5
- attn_weight: bfloat16 [4, 768, 768], P(None, None, 'col'), may hold values from -0.21875 to 0.21875
- out_weight: bfloat16 [768, 768], P('col'), may hold values from -0.21875 to 0.21875
- cotangent: bfloat16 [24, 128, 768], P(('group', 'row')), may hold values from -6 to 6
Outputs:
- pair_next: bfloat16 [128, 128, 128], P(('group', 'row'), 'col')
- pair_grad: float32 [128, 128, 128], P(('group', 'row'), 'col')
- bias_weight_grad: float32 [128, 16], replicated
- denoised: bfloat16 [24, 128, 768], P(('group', 'row'), 'col')
- token_grad: bfloat16 [24, 128, 768], P(('group', 'row'), 'col')
- attn_weight_grad: float32 [4, 768, 768], P(None, ('group', 'row'), 'col')
- out_weight_grad: float32 [768, 768], P('col', ('group', 'row'))
Inputs may be any that keep to these rules, and one draw needn't show every extreme that they name: `chain_id`: chain numbers never fall along the tokens.
All inputs are finite; a program needn't handle non-finite values. No bound on the sum of `pair_mask` on one device may be relied on, other than what follows from the above.
Results may differ from a plain program's by a relative error of at most 0.014.
Values may be sent and summed in bfloat16 or wider, within the bound.
No kernel may reach another device: no remote copies, remote signals or barrier semaphores. Data moves between devices by JAX's collectives and lax.ppermute only.
A program may use at most 64 MiB of HBM per device.

v0:
```python
import functools
import math

import jax
import jax.numpy as jnp
from jax import lax
from jax.experimental import pallas as pl
from jax.experimental.pallas import tpu as pltpu
from jax.sharding import PartitionSpec as P


LEVELS = 200


EPSILON = 1e-05
SIGMA_LOW = 0.1
SIGMA_SPAN = 100.0


def normalize(values):
    average = jnp.mean(values, -1, keepdims=True)
    centred = values - average
    return centred * lax.rsqrt(jnp.mean(centred * centred, -1, keepdims=True) + EPSILON)


def norm_back(gradient, values, norm_gain):
    average = jnp.mean(values, -1, keepdims=True)
    centred = values - average
    inverse = lax.rsqrt(jnp.mean(centred * centred, -1, keepdims=True) + EPSILON)
    normed = centred * inverse
    weighted = gradient * norm_gain
    return inverse * (
        weighted
        - jnp.mean(weighted, -1, keepdims=True)
        - normed * jnp.mean(weighted * normed, -1, keepdims=True)
    )


def noise_scale(levels):
    sigma_vals = SIGMA_LOW * SIGMA_SPAN ** (levels.astype(jnp.float32) / (LEVELS - 1))
    return lax.rsqrt(1.0 + sigma_vals * sigma_vals)


def general_shards(
    pair_repr,
    pair_mask,
    chain_id,
    tri_in_gain,
    tri_proj,
    tri_gate,
    tri_out_gain,
    tri_out,
    bias_gain,
    bias_weight,
    chain_bias,
    tokens,
    noise_level,
    attn_gain,
    attn_weight,
    out_weight,
    cotangent,
):
    rows_here = pair_repr.shape[0]
    cols_here = pair_repr.shape[1]
    channels = pair_repr.shape[2]
    token_count = chain_id.shape[0]
    heads_all = bias_weight.shape[1]
    hidden_width = attn_gain.shape[0]
    head_size = hidden_width // heads_all
    inverse_square_root = 1.0 / math.sqrt(head_size)
    row_index = lax.axis_index(("group", "row"))
    col_index = lax.axis_index("col")
    pair_tile = pair_repr.astype(jnp.float32)
    pair_in = (normalize(pair_tile) * tri_in_gain).astype(jnp.bfloat16)
    flat_in = pair_in.reshape(-1, channels)
    projected = jnp.dot(flat_in, tri_proj, preferred_element_type=jnp.float32).reshape(
        rows_here, cols_here, 4, channels
    )
    mask_tile = pair_mask.astype(jnp.float32)[:, :, None]
    left_proj = (jax.nn.sigmoid(projected[:, :, 0]) * projected[:, :, 1] * mask_tile).astype(
        jnp.bfloat16
    )
    right_proj = (jax.nn.sigmoid(projected[:, :, 2]) * projected[:, :, 3] * mask_tile).astype(
        jnp.bfloat16
    )
    gate_act = jax.nn.sigmoid(
        jnp.dot(flat_in, tri_gate, preferred_element_type=jnp.float32)
    ).reshape(rows_here, cols_here, channels)
    left_major = jnp.transpose(left_proj, (2, 0, 1))
    right_major = jnp.transpose(right_proj, (2, 0, 1))
    partial_rows = jnp.einsum(
        "cjk,cik->cji",
        lax.all_gather(right_major, ("group", "row"), axis=1, tiled=True),
        left_major,
        preferred_element_type=jnp.float32,
    )
    summed = lax.psum_scatter(partial_rows, "col", scatter_dimension=1, tiled=True)
    triangle = jnp.transpose(summed, (2, 1, 0))
    tri_normed = (normalize(triangle) * tri_out_gain).astype(jnp.bfloat16)
    update = jnp.dot(
        tri_normed.reshape(-1, channels), tri_out, preferred_element_type=jnp.float32
    ).reshape(rows_here, cols_here, channels)
    updated = pair_tile + gate_act * update
    bias_in = (normalize(updated) * bias_gain).astype(jnp.bfloat16)
    flat_bias = bias_in.reshape(-1, channels)
    bias_tile = jnp.dot(flat_bias, bias_weight, preferred_element_type=jnp.float32).reshape(
        rows_here, cols_here, heads_all
    )
    row_chain = lax.dynamic_slice_in_dim(chain_id, row_index * rows_here, rows_here)
    col_chain = lax.dynamic_slice_in_dim(chain_id, col_index * cols_here, cols_here)
    same_chain = (row_chain[:, None] == col_chain[None, :]).astype(jnp.float32)
    bias_tile = bias_tile + same_chain[:, :, None] * chain_bias
    bias_major = jnp.transpose(bias_tile.astype(jnp.bfloat16), (2, 0, 1))
    head_rows = lax.all_to_all(bias_major, "col", split_axis=0, concat_axis=2, tiled=True)
    per_head_bias = lax.all_gather(head_rows, ("group", "row"), axis=1, tiled=True).astype(
        jnp.float32
    )
    local_heads = per_head_bias.shape[0]
    scales = noise_scale(noise_level)

    def one_copy(carried, inputs):
        bias_sums, weight_sums, output_sums = carried
        token_rows, cot_rows, scaling = inputs
        sequence_length = token_rows.shape[0]
        scaled = scaling * token_rows.astype(jnp.float32)
        hidden = (normalize(scaled) * attn_gain).astype(jnp.bfloat16)
        projections = jnp.einsum(
            "nd,gde->gne", hidden, attn_weight, preferred_element_type=jnp.float32
        )
        query_rows = (
            projections[0].astype(jnp.bfloat16).reshape(sequence_length, local_heads, head_size)
        )
        key_matrix = (
            projections[1].astype(jnp.bfloat16).reshape(sequence_length, local_heads, head_size)
        )
        value_rows = (
            projections[2].astype(jnp.bfloat16).reshape(sequence_length, local_heads, head_size)
        )
        gate_sig = jax.nn.sigmoid(projections[3])
        logit_scores = (
            jnp.einsum("fuc,suc->ufs", query_rows, key_matrix, preferred_element_type=jnp.float32)
            * inverse_square_root
            + per_head_bias
        )
        exponent = jnp.exp(logit_scores)
        attention = exponent / jnp.sum(exponent, -1, keepdims=True)
        attention_probs = attention.astype(jnp.bfloat16)
        attended_rows = jnp.einsum(
            "vkq,qvy->kvy", attention_probs, value_rows, preferred_element_type=jnp.float32
        ).reshape(sequence_length, -1)
        gated_out = (gate_sig * attended_rows).astype(jnp.bfloat16)
        grad_gated = jnp.dot(cot_rows, out_weight.T, preferred_element_type=jnp.float32)
        grad_gate = grad_gated * attended_rows * gate_sig * (1.0 - gate_sig)
        attended_gradient = (
            (grad_gated * gate_sig)
            .astype(jnp.bfloat16)
            .reshape(sequence_length, local_heads, head_size)
        )
        probability_gradient = jnp.einsum(
            "fuc,suc->ufs", attended_gradient, value_rows, preferred_element_type=jnp.float32
        )
        value_gradient = jnp.einsum(
            "avj,vat->jat", attention_probs, attended_gradient, preferred_element_type=jnp.float32
        )
        grad_score = attention * (
            probability_gradient - jnp.sum(attention * probability_gradient, -1, keepdims=True)
        )
        score_gradient = grad_score.astype(jnp.bfloat16)
        query_gradient = (
            jnp.einsum(
                "vkq,qvy->kvy", score_gradient, key_matrix, preferred_element_type=jnp.float32
            )
            * inverse_square_root
        )
        key_gradient = (
            jnp.einsum(
                "avj,vat->jat", score_gradient, query_rows, preferred_element_type=jnp.float32
            )
            * inverse_square_root
        )
        grads = jnp.stack(
            [
                query_gradient.reshape(sequence_length, -1),
                key_gradient.reshape(sequence_length, -1),
                value_gradient.reshape(sequence_length, -1),
                grad_gate,
            ]
        ).astype(jnp.bfloat16)
        weight_sums = weight_sums + jnp.einsum(
            "nd,gne->gde", hidden, grads, preferred_element_type=jnp.float32
        )
        output_sums = output_sums + jnp.dot(
            gated_out.T, cot_rows, preferred_element_type=jnp.float32
        )
        return ((bias_sums + grad_score, weight_sums, output_sums), (gated_out, grads))

    start_sums = (
        jnp.zeros((local_heads, token_count, token_count), jnp.float32),
        jnp.zeros(attn_weight.shape, jnp.float32),
        jnp.zeros(out_weight.shape, jnp.float32),
    )
    final_sums, stacked = lax.scan(one_copy, start_sums, (tokens, cotangent, scales))
    bias_sums, weight_sums, output_sums = final_sums
    gated_all, grads_all = stacked
    token_share = token_count // lax.axis_size("col")
    attn_parts = jnp.einsum(
        "tnd,de->tne", gated_all, out_weight, preferred_element_type=jnp.float32
    )
    hidden_parts = jnp.einsum(
        "tgne,gde->tnd", grads_all, attn_weight, preferred_element_type=jnp.float32
    )
    attn_out, grad_hidden = (
        lax.psum_scatter(attn_parts, "col", scatter_dimension=1, tiled=True),
        lax.psum_scatter(hidden_parts, "col", scatter_dimension=1, tiled=True),
    )
    first_token = col_index * token_share
    token_mine = lax.dynamic_slice_in_dim(tokens, first_token, token_share, 1)
    cot_mine = lax.dynamic_slice_in_dim(cotangent, first_token, token_share, 1)
    scaled_mine = scales[:, None, None] * token_mine.astype(jnp.float32)
    denoised = (scaled_mine + attn_out).astype(jnp.bfloat16)
    grad_scaled = cot_mine.astype(jnp.float32) + norm_back(grad_hidden, scaled_mine, attn_gain)
    token_grad = (scales[:, None, None] * grad_scaled).astype(jnp.bfloat16)
    bias_rows_sum, out_grad, weight_grad = (
        lax.psum_scatter(bias_sums, ("group", "row"), scatter_dimension=1, tiled=True),
        lax.psum_scatter(output_sums, ("group", "row"), scatter_dimension=1, tiled=True),
        lax.psum_scatter(weight_sums, ("group", "row"), scatter_dimension=1, tiled=True),
    )
    bias_back = lax.all_to_all(bias_rows_sum, "col", split_axis=2, concat_axis=0, tiled=True)
    grad_bias = jnp.transpose(bias_back, (1, 2, 0)).reshape(-1, heads_all)
    grad_in = jnp.dot(
        grad_bias, bias_weight.astype(jnp.float32).T, precision=lax.Precision.HIGHEST
    ).reshape(rows_here, cols_here, channels)
    pair_grad = norm_back(grad_in, updated, bias_gain)
    weight_part = jnp.dot(
        flat_bias.astype(jnp.float32).T, grad_bias, precision=lax.Precision.HIGHEST
    )
    bias_weight_grad = lax.psum(weight_part, ("group", "row", "col"))
    return (
        updated.astype(jnp.bfloat16),
        pair_grad,
        bias_weight_grad,
        denoised,
        token_grad,
        weight_grad,
        out_grad,
    )


LANES = 128


def dot_nn(a, b, **kw):
    return lax.dot_general(a, b, (((1,), (0,)), ((), ())), preferred_element_type=jnp.float32, **kw)


def dot_nt(a, b, **kw):
    return lax.dot_general(a, b, (((1,), (1,)), ((), ())), preferred_element_type=jnp.float32, **kw)


def dot_tn(a, b, **kw):
    return lax.dot_general(a, b, (((0,), (0,)), ((), ())), preferred_element_type=jnp.float32, **kw)


def turn(values, groups, width):
    shift = (groups * width) % LANES
    return values if shift == 0 else pltpu.roll(values, shift, 1)


def merge(pieces, lane_group):
    merged = pieces[0]
    for g in range(1, len(pieces)):
        merged = jnp.where(lane_group == g, pieces[g], merged)
    return merged


def lane_groups(rows, width):
    return lax.broadcasted_iota(jnp.int32, (rows, LANES), 1) // width


def channel_order(channels, devices):
    r = lax.broadcasted_iota(jnp.int32, (channels, channels), 0)
    c = lax.broadcasted_iota(jnp.int32, (channels, channels), 1)
    return (r % devices) * (channels // devices) + r // devices == c


def whole(shape, dtype):
    return jax.ShapeDtypeStruct(shape, dtype)


def far(values):
    return pltpu.with_memory_space_constraint(values, pltpu.HBM)


def pair_in_kernel(pair_ref, mask_ref, gain_ref, proj_ref, out_ref, rows_ref):
    devices = out_ref.shape[0]
    rows, width = mask_ref.shape
    channels = pair_ref.shape[1]
    groups = LANES // width
    pair_in = (normalize(pair_ref[...].astype(jnp.float32)) * gain_ref[...]).astype(jnp.bfloat16)
    order = channel_order(channels, devices).astype(jnp.float32).astype(jnp.bfloat16)
    lanes = lane_groups(devices, width)
    mask = jnp.concatenate([mask_ref[...].astype(jnp.float32)] * groups, axis=1)
    for side in range(2):
        first = 2 * side * channels
        gate_t = dot_nt(order, proj_ref[:, first : first + channels]).astype(jnp.bfloat16)
        value_t = dot_nt(order, proj_ref[:, first + channels : first + 2 * channels]).astype(
            jnp.bfloat16
        )
        product = jax.nn.sigmoid(dot_nt(gate_t, pair_in)) * dot_nt(value_t, pair_in)
        for i in range(rows):
            q, s = divmod(i, groups)
            tile = merge(
                [
                    turn(
                        product[g * devices : (g + 1) * devices, q * LANES : (q + 1) * LANES],
                        g - s,
                        width,
                    )
                    for g in range(groups)
                ],
                lanes,
            )
            rows_ref[pl.ds(i, devices, stride=rows), :] = tile * mask[i : i + 1]
        out_ref[:, side] = rows_ref[...].astype(jnp.bfloat16).reshape(devices, rows, LANES)


def triangle_kernel(in_ref, out_ref, *, width):
    stripes, cols, _, rows, _ = in_ref.shape
    groups = LANES // width
    tokens = stripes * rows
    lanes = lane_groups(tokens, width)
    totals = [jnp.zeros((tokens, LANES), jnp.float32) for _ in range(groups)]
    for col in range(cols):
        left = in_ref[:, col, 0].reshape(tokens, LANES)
        right = in_ref[:, col, 1].reshape(tokens, LANES)
        for g in range(groups):
            totals[g] += dot_nt(jnp.where(lanes == g, left, jnp.zeros_like(left)), right)
    for col in range(cols):
        out_ref[:, col] = (
            merge([turn(totals[g], g - col, width) for g in range(groups)], lanes)
            .astype(jnp.bfloat16)
            .reshape(stripes, rows, LANES)
        )


def pair_out_kernel(
    here_ref,
    chain_ref,
    in_ref,
    pair_ref,
    chain_row_ref,
    in_gain_ref,
    gate_ref,
    out_gain_ref,
    out_weight_ref,
    bias_gain_ref,
    bias_weight_ref,
    chain_bias_ref,
    next_ref,
    updated_ref,
    bias_ref,
    rows_ref,
    *,
    width,
):
    devices, rows, _ = in_ref.shape
    stripes, cols = bias_ref.shape[:2]
    channels = pair_ref.shape[1]
    heads = bias_weight_ref.shape[0]
    groups = LANES // width

    def all_lanes(sums):
        total = sums
        for g in range(1, groups):
            total = total + turn(sums, g, width)
        return total

    triangle = in_ref[...].astype(jnp.float32)
    average = all_lanes(jnp.sum(triangle, 0)) * (1.0 / channels)
    centred = triangle - average
    inverse = lax.rsqrt(all_lanes(jnp.sum(centred * centred, 0)) * (1.0 / channels) + EPSILON)
    rows_ref[...] = (centred * inverse).reshape(devices * rows, LANES)
    lanes = lane_groups(devices, width)
    blocks = []
    for q in range(rows // groups):
        tiles = [
            rows_ref[pl.ds(q * groups + s, devices, stride=rows), :] for s in range(groups)
        ]
        blocks.append(
            jnp.concatenate(
                [
                    merge([turn(tiles[s], s - g, width) for s in range(groups)], lanes)
                    for g in range(groups)
                ],
                axis=0,
            )
        )
    normed_t = jnp.concatenate(blocks, axis=1)
    order = channel_order(channels, devices)
    gain_t = jnp.sum(jnp.where(order, out_gain_ref[...], 0.0), axis=1, keepdims=True)
    order_b = order.astype(jnp.float32).astype(jnp.bfloat16)
    weight = dot_nn(order_b, out_weight_ref[...]).astype(jnp.bfloat16)
    update = dot_tn((normed_t * gain_t).astype(jnp.bfloat16), weight)
    pair = pair_ref[...].astype(jnp.float32)
    pair_in = (normalize(pair) * in_gain_ref[...]).astype(jnp.bfloat16)
    updated = pair + jax.nn.sigmoid(dot_nn(pair_in, gate_ref[...])) * update
    updated_ref[...] = updated
    next_ref[...] = updated.astype(jnp.bfloat16)
    bias_in = (normalize(updated) * bias_gain_ref[...]).astype(jnp.bfloat16)
    unit = lax.broadcasted_iota(jnp.int32, (heads, heads), 0) == lax.broadcasted_iota(
        jnp.int32, (heads, heads), 1
    )
    chain_t = jnp.sum(jnp.where(unit, chain_bias_ref[...], 0.0), axis=1, keepdims=True)
    bias_t = dot_nt(bias_weight_ref[...], bias_in)
    lanes_h = lane_groups(heads, width)
    chain_row = jnp.broadcast_to(chain_row_ref[...], (heads, LANES))
    col_chain = merge(
        [
            pltpu.roll(chain_row, (g + cols - here_ref[1]) % cols * width, 1)
            for g in range(groups)
        ],
        lanes_h,
    )
    head_group = lax.broadcasted_iota(jnp.int32, (heads, LANES), 0) % groups
    spread = []
    for i in range(rows):
        q, s = divmod(i, groups)
        block = bias_t[:, q * LANES : (q + 1) * LANES]
        tile = jnp.zeros_like(block)
        for g in range(groups):
            tile = jnp.where(
                (lanes_h == g) & (head_group == g), turn(block, g - s, width), tile
            )
        row_chain = chain_ref[here_ref[0] * rows + i]
        extra = jnp.where((col_chain == row_chain) & (lanes_h == head_group), chain_t, 0.0)
        spread.append(tile + extra)
    spread = jnp.concatenate(spread, axis=0).astype(jnp.bfloat16)
    packed = dot_nn(head_gather(rows, cols, heads).astype(jnp.bfloat16), spread)
    packed = packed.astype(jnp.bfloat16).reshape(cols, rows, LANES)
    for stripe in range(stripes):
        bias_ref[stripe] = packed


def head_gather(rows, cols, heads):
    a = lax.broadcasted_iota(jnp.int32, (cols * rows, rows * heads), 0)
    b = lax.broadcasted_iota(jnp.int32, (cols * rows, rows * heads), 1)
    return ((a % rows == b // heads) & (a // rows == (b % heads) // (heads // cols))).astype(
        jnp.float32
    )


def token_in_kernel(
    scale_ref,
    tokens_ref,
    cot_ref,
    gain_ref,
    weight_ref,
    out_weight_ref,
    query_ref,
    key_ref,
    value_ref,
    gated_ref,
    sig_ref,
    grad_ref,
    score_ref,
    prob_ref,
    hidden_t_ref,
    cot_t_ref,
    hidden_ref,
    *,
    head_size,
):
    copies, length, _ = tokens_ref.shape
    inner = query_ref.shape[1]
    inverse_square_root = 1.0 / math.sqrt(head_size)
    for t in range(copies):
        part = slice(t * length, (t + 1) * length)
        scaled = scale_ref[t] * tokens_ref[t].astype(jnp.float32)
        hidden = normalize(scaled) * gain_ref[...]
        hidden_ref[part] = hidden.astype(jnp.bfloat16)
        hidden_t_ref[:, part] = hidden.T.astype(jnp.bfloat16)
        cot_t_ref[:, part] = cot_ref[t].astype(jnp.float32).T.astype(jnp.bfloat16)
    hidden = hidden_ref[...]
    query_ref[...] = dot_nt(hidden, weight_ref[0]).astype(jnp.bfloat16)
    key_ref[...] = dot_nt(hidden, weight_ref[1]).astype(jnp.bfloat16)
    value_ref[...] = dot_nt(hidden, weight_ref[2]).astype(jnp.bfloat16)
    sig = jax.nn.sigmoid(dot_nt(hidden, weight_ref[3]))
    sig_ref[...] = sig
    grad = dot_nt(cot_ref[...].reshape(copies * length, -1), out_weight_ref[...])
    grad_ref[...] = grad
    gated_ref[...] = (grad * sig).astype(jnp.bfloat16)
    head_of = lax.broadcasted_iota(jnp.int32, (length, inner), 1) // head_size
    for t in range(copies):
        part = slice(t * length, (t + 1) * length)
        query, key_rows, value, gated = (
            r[part] for r in (query_ref, key_ref, value_ref, gated_ref)
        )
        for h in range(score_ref.shape[1]):
            mine = head_of == h
            query_h = jnp.where(mine, query, jnp.zeros_like(query))
            gated_h = jnp.where(mine, gated, jnp.zeros_like(gated))
            score_ref[t, h] = dot_nt(query_h, key_rows) * inverse_square_root
            prob_ref[t, h] = dot_nt(gated_h, value)


def attention_kernel(
    here_ref,
    bias_ref,
    query_ref,
    key_ref,
    value_ref,
    gated_ref,
    sig_ref,
    grad_ref,
    score_ref,
    prob_ref,
    weight_ref,
    out_weight_ref,
    pair_ref,
    outs_ref,
    grads_ref,
    *refs,
    width,
    head_size,
):
    part_refs, (sums_ref, parts_ref) = refs[:-2], refs[-2:]
    stripes, cols, rows, _ = bias_ref.shape
    copies, heads, length, _ = score_ref.shape
    inner, hidden_width = out_weight_ref.shape
    share = length // cols
    lanes = lane_groups(length, width)
    head_of = lax.broadcasted_iota(jnp.int32, (length, inner), 1) // head_size
    inverse_square_root = 1.0 / math.sqrt(head_size)
    tiles = [
        bias_ref[:, col].astype(jnp.float32).reshape(length, LANES) for col in range(cols)
    ]
    bias = [
        merge([turn(tiles[col], col - h, width) for col in range(cols)], lanes)
        for h in range(heads)
    ]
    for t in range(copies):
        part = slice(t * length, (t + 1) * length)
        query, key_rows, value, gated = (
            r[part] for r in (query_ref, key_ref, value_ref, gated_ref)
        )
        attended = jnp.zeros((length, inner), jnp.float32)
        grad_query, grad_key, grad_value = attended, attended, attended
        for h in range(heads):
            mine = head_of == h
            query_h, key_h, value_h, gated_h = (
                jnp.where(mine, r, jnp.zeros_like(r)) for r in (query, key_rows, value, gated)
            )
            exponent = jnp.exp(score_ref[t, h] + bias[h])
            attention = exponent / jnp.sum(exponent, -1, keepdims=True)
            attention_b = attention.astype(jnp.bfloat16)
            grad_prob = prob_ref[t, h]
            grad_score = attention * (
                grad_prob - jnp.sum(attention * grad_prob, -1, keepdims=True)
            )
            sums_ref[h] = grad_score if t == 0 else sums_ref[h] + grad_score
            score_b = grad_score.astype(jnp.bfloat16)
            attended += dot_nn(attention_b, value_h)
            grad_query += dot_nn(score_b, key_h)
            grad_key += dot_tn(score_b, query_h)
            grad_value += dot_tn(attention_b, gated_h)
        sig = sig_ref[part]
        gated_out = (sig * attended).astype(jnp.bfloat16)
        grads = [
            (grad_query * inverse_square_root).astype(jnp.bfloat16),
            (grad_key * inverse_square_root).astype(jnp.bfloat16),
            grad_value.astype(jnp.bfloat16),
            (grad_ref[part] * attended * sig * (1.0 - sig)).astype(jnp.bfloat16),
        ]
        outs_ref[part] = gated_out
        for g in range(4):
            grads_ref[g, part] = grads[g]
        out_part = dot_nn(gated_out, out_weight_ref[...])
        in_part = dot_nn(grads[0], weight_ref[0])
        for g in range(1, 4):
            in_part += dot_nn(grads[g], weight_ref[g])
        parts_ref[:, 0, t] = out_part.astype(jnp.bfloat16).reshape(cols, share, hidden_width)
        parts_ref[:, 1, t] = in_part.astype(jnp.bfloat16).reshape(cols, share, hidden_width)
    for k in range(cols):
        part_refs[k][...] = parts_ref[(here_ref[1] + k) % cols]
    for col in range(cols):
        pair_ref[:, col] = (
            merge([turn(sums_ref[h], h - col, width) for h in range(heads)], lanes)
            .astype(jnp.bfloat16)
            .reshape(stripes, rows, LANES)
        )


def weight_in_kernel(
    here_ref, hidden_t_ref, cot_t_ref, grads_ref, outs_ref, keep_ref, send_ref, wire_ref
):
    hidden_t = hidden_t_ref[...]
    chips, _, block, _ = wire_ref.shape

    def put(values, first, last):
        wire_ref[:, :, :, first * LANES : last * LANES] = values.astype(jnp.bfloat16).reshape(
            chips, 2, block, -1
        )

    weights = [dot_nn(hidden_t, grads_ref[g]) for g in range(4)]
    weights.append(dot_nn(cot_t_ref[...], outs_ref[...]))
    for g in range(5):
        put(weights[g][:, :LANES], g, g + 1)
    tails = [w[:, LANES:] for w in weights]
    tails.append(jnp.zeros_like(tails[0]))
    for g in range(3):
        put(jnp.concatenate(tails[2 * g : 2 * g + 2], axis=1), 5 + g, 6 + g)
    core = here_ref[0] % 2
    keep_ref[...] = wire_ref[:, core]
    send_ref[...] = wire_ref[:, 1 - core]


def weight_add_kernel(here_ref, keep_ref, got_ref, *refs):
    out_refs, sum_ref = refs[:-1], refs[-1]
    sum_ref[...] = (
        keep_ref[...].astype(jnp.float32) + got_ref[...].astype(jnp.float32)
    ).astype(jnp.bfloat16)
    chip = here_ref[0] // 2
    for k in range(len(out_refs)):
        out_refs[k][...] = sum_ref[chip ^ k]


def pair_back_kernel(
    in_ref, updated_ref, gain_ref, bias_weight_ref, grad_ref, weight_ref, *, width
):
    _, cols, rows, _ = in_ref.shape
    heads = bias_weight_ref.shape[0]
    groups = LANES // width
    total = jnp.sum(in_ref[...].astype(jnp.float32), 0).reshape(cols * rows, LANES)
    spread = dot_tn(head_gather(rows, cols, heads), total, precision=lax.Precision.HIGHEST)
    lanes = lane_groups(heads, width)
    head_group = lax.broadcasted_iota(jnp.int32, (heads, LANES), 0) % groups
    blocks = []
    for q in range(rows // groups):
        tiles = []
        for s in range(groups):
            i = q * groups + s
            tile = spread[i * heads : (i + 1) * heads]
            turned = tile
            for g in range(groups):
                turned = jnp.where(head_group == g, turn(tile, s - g, width), turned)
            tiles.append(turned)
        blocks.append(merge(tiles, lanes))
    grad_t = jnp.concatenate(blocks, axis=1)
    updated = updated_ref[...]
    gain = gain_ref[...]
    grad_in = lax.dot_general(
        grad_t,
        bias_weight_ref[...].astype(jnp.float32),
        (((0,), (0,)), ((), ())),
        precision=lax.Precision.HIGHEST,
        preferred_element_type=jnp.float32,
    )
    grad_ref[...] = norm_back(grad_in, updated, gain)
    bias_in = (normalize(updated) * gain).astype(jnp.bfloat16).astype(jnp.float32)
    weight = dot_nn(grad_t, bias_in, precision=lax.Precision.HIGHEST).astype(jnp.bfloat16)
    for device in range(weight_ref.shape[0]):
        weight_ref[device] = weight


def token_out_kernel(here_ref, scale_ref, tokens_ref, cot_ref, gain_ref, *refs):
    part_refs, (out_ref, grad_ref) = refs[:-2], refs[-2:]
    for t in range(out_ref.shape[0]):
        sums = part_refs[0][:, t].astype(jnp.float32)
        for r in part_refs[1:]:
            sums = sums + r[:, t].astype(jnp.float32)
        scale = scale_ref[t]
        scaled = scale * tokens_ref[t].astype(jnp.float32)
        out_ref[t] = (scaled + sums[0]).astype(jnp.bfloat16)
        grad = cot_ref[t].astype(jnp.float32) + norm_back(sums[1], scaled, gain_ref[...])
        grad_ref[t] = (scale * grad).astype(jnp.bfloat16)


def weight_out_kernel(*refs):
    in_refs, (grad_ref, out_ref) = refs[:-2], refs[-2:]
    total = in_refs[0][...].astype(jnp.float32)
    for r in in_refs[1:]:
        total = total + r[...].astype(jnp.float32)
    half = LANES // 2
    for g in range(4):
        grad_ref[g, :, :LANES] = total[:, g * LANES : (g + 1) * LANES]
        first = (5 + g // 2) * LANES + (g % 2) * half
        grad_ref[g, :, LANES:] = total[:, first : first + half]
    rows = jnp.concatenate(
        [total[:, 4 * LANES : 5 * LANES], total[:, 7 * LANES : 8 * LANES]], axis=1
    )
    out_ref[...] = rows.T[: out_ref.shape[0]]


def fits(pair_repr, token_count, heads_all, inner, hidden_width, stripes, cols):
    rows, width, channels = pair_repr.shape
    groups = LANES // width if LANES % width == 0 else 0
    return (
        groups > 0
        and token_count == LANES
        and channels == LANES
        and channels == stripes * cols * groups
        and cols == groups
        and heads_all == cols * groups
        and rows % 16 == 0
        and stripes * rows == token_count
        and stripes % 2 == 0
        and stripes & (stripes - 1) == 0
        and inner == LANES + LANES // 2
        and hidden_width % (16 * stripes) == 0
    )


def shards(
    pair_repr,
    pair_mask,
    chain_id,
    tri_in_gain,
    tri_proj,
    tri_gate,
    tri_out_gain,
    tri_out,
    bias_gain,
    bias_weight,
    chain_bias,
    tokens,
    noise_level,
    attn_gain,
    attn_weight,
    out_weight,
    cotangent,
):
    stripe_axes = ("group", "row")
    all_axes = ("group", "row", "col")
    stripes = lax.axis_size(stripe_axes)
    cols = lax.axis_size("col")
    rows, width, channels = pair_repr.shape
    heads_all = bias_weight.shape[1]
    copies, length, hidden_width = tokens.shape
    inner = attn_weight.shape[2]
    if not fits(pair_repr, length, heads_all, inner, hidden_width, stripes, cols):
        return general_shards(
            pair_repr,
            pair_mask,
            chain_id,
            tri_in_gain,
            tri_proj,
            tri_gate,
            tri_out_gain,
            tri_out,
            bias_gain,
            bias_weight,
            chain_bias,
            tokens,
            noise_level,
            attn_gain,
            attn_weight,
            out_weight,
            cotangent,
        )
    head_size = hidden_width // heads_all
    devices = stripes * cols
    pairs = rows * width
    bf16, f32 = jnp.bfloat16, jnp.float32
    vmem = pl.BlockSpec(memory_space=pltpu.VMEM)
    smem = pl.BlockSpec(memory_space=pltpu.SMEM)
    row_index = lax.axis_index(stripe_axes)
    col_index = lax.axis_index("col")
    here = jnp.stack([row_index, col_index]).astype(jnp.int32)
    pair_flat = pair_repr.reshape(pairs, channels)
    scales = noise_scale(noise_level)
    weight_t = jnp.swapaxes(attn_weight, 1, 2)
    bias_weight_t = bias_weight.T

    def call(kernel, mib, out_shape, n_smem, n_vmem, scratch=(), **options):
        many = isinstance(out_shape, tuple)
        return pl.pallas_call(
            functools.partial(kernel, **options),
            out_shape=out_shape,
            in_specs=[smem] * n_smem + [vmem] * n_vmem,
            out_specs=(vmem,) * len(out_shape) if many else vmem,
            scratch_shapes=list(scratch),
            compiler_params=pltpu.CompilerParams(vmem_limit_bytes=mib << 20),
        )

    def exchange(values, axes):
        return lax.all_to_all(values, axes, 0, 0, tiled=True)

    def shift(values, k):
        return lax.ppermute(values, "col", [(i, (i + k) % cols) for i in range(cols)])

    projected = call(
        pair_in_kernel,
        8,
        whole((devices, 2, rows, LANES), bf16),
        0,
        4,
        [pltpu.VMEM((devices * rows, LANES), f32)],
    )(far(pair_flat), far(pair_mask), far(tri_in_gain[None]), far(tri_proj))
    sides = exchange(projected.reshape(devices, 2 * rows, LANES), all_axes)
    tall = copies * length
    local = heads_all // cols
    query, key_rows, value, gated, gate_sig, grad_gated, scores, probs, hidden_t, cot_t = call(
        token_in_kernel,
        16,
        (
            *[pltpu.HBM((tall, inner), bf16)] * 4,
            *[pltpu.HBM((tall, inner), f32)] * 2,
            *[pltpu.HBM((copies, local, length, length), f32)] * 2,
            *[pltpu.HBM((hidden_width, tall), bf16)] * 2,
        ),
        1,
        5,
        [pltpu.VMEM((tall, hidden_width), bf16)],
        head_size=head_size,
    )(
        scales, *map(far, (tokens, cotangent, attn_gain[None], weight_t, out_weight))
    )
    triangle = call(
        triangle_kernel, 8, whole((stripes, cols, rows, LANES), bf16), 0, 1, width=width
    )(sides.reshape(stripes, cols, 2, rows, LANES))
    triangle = exchange(triangle.reshape(devices, rows, LANES), all_axes)
    pair_next, updated, bias_tile = call(
        pair_out_kernel,
        8,
        (
            pltpu.HBM((pairs, channels), bf16),
            pltpu.HBM((pairs, channels), f32),
            whole((stripes, cols, rows, LANES), bf16),
        ),
        2,
        10,
        [pltpu.VMEM((devices * rows, LANES), f32)],
        width=width,
    )(
        here,
        chain_id,
        triangle,
        *map(
            far,
            (
                pair_flat,
                chain_id[None],
                tri_in_gain[None],
                tri_gate,
                tri_out_gain[None],
                tri_out,
                bias_gain[None],
                bias_weight_t,
                chain_bias[None],
            ),
        ),
    )
    head_bias = exchange(bias_tile.reshape(devices, rows, LANES), all_axes)
    part = pltpu.HBM((2, copies, length // cols, hidden_width), bf16)
    bias_sums, outs, grads, *parts = call(
        attention_kernel,
        20,
        (
            whole((stripes, cols, rows, LANES), bf16),
            pltpu.HBM((tall, inner), bf16),
            pltpu.HBM((4, tall, inner), bf16),
            *[part] * cols,
        ),
        1,
        11,
        [
            pltpu.VMEM((local, length, length), f32),
            pltpu.VMEM((cols, 2, copies, length // cols, hidden_width), bf16),
        ],
        width=width,
        head_size=head_size,
    )(
        here,
        head_bias.reshape(stripes, cols, rows, LANES),
        *map(
            far,
            (
                query,
                key_rows,
                value,
                gated,
                gate_sig,
                grad_gated,
                scores,
                probs,
                weight_t,
                out_weight,
            ),
        ),
    )
    bias_back = exchange(bias_sums.reshape(devices, rows, LANES), all_axes)
    received = [parts[0]] + [shift(parts[k], k) for k in range(1, cols)]
    chips = stripes // 2
    block = hidden_width // stripes
    keep, give = call(
        weight_in_kernel,
        16,
        (pltpu.HBM((chips, block, 8 * LANES), bf16),) * 2,
        1,
        4,
        [pltpu.VMEM((chips, 2, block, 8 * LANES), bf16)],
    )(here, *map(far, (hidden_t, cot_t, grads, outs)))
    got = lax.ppermute(give, stripe_axes, [(i, i ^ 1) for i in range(stripes)])
    mine, *give = call(
        weight_add_kernel,
        12,
        (pltpu.HBM((block, 8 * LANES), bf16),) * chips,
        1,
        2,
        [pltpu.VMEM((chips, block, 8 * LANES), bf16)],
    )(here, far(keep), got)
    wires = [mine]
    for k in range(1, chips):
        wires.append(
            lax.ppermute(
                give[k - 1], stripe_axes, [(i, i ^ (2 * k)) for i in range(stripes)]
            )
        )
    pair_grad, weight_part = call(
        pair_back_kernel,
        8,
        (whole((pairs, channels), f32), whole((devices, heads_all, channels), bf16)),
        0,
        4,
        width=width,
    )(
        bias_back.reshape(stripes, cols, rows, LANES),
        *map(far, (updated, bias_gain[None], bias_weight_t)),
    )
    weight_part = exchange(weight_part, all_axes)
    bias_weight_grad = jnp.sum(weight_part.astype(f32), 0).T
    weight_grad, out_grad = call(
        weight_out_kernel,
        16,
        (
            whole((4, hidden_width // stripes, inner), f32),
            whole((inner, hidden_width // stripes), f32),
        ),
        0,
        chips,
    )(far(wires[0]), *wires[1:])
    share = length // cols
    mine = pl.BlockSpec((copies, share, hidden_width), lambda i, here: (0, here[1], 0))
    fixed = lambda shape: pl.BlockSpec(shape, lambda i, here: (0,) * len(shape))
    denoised, token_grad = pl.pallas_call(
        token_out_kernel,
        grid_spec=pltpu.PrefetchScalarGridSpec(
            num_scalar_prefetch=1,
            grid=(1,),
            in_specs=[smem, mine, mine, fixed((1, hidden_width))] + [fixed((2, copies, share, hidden_width))] * cols,
            out_specs=[fixed((copies, share, hidden_width))] * 2,
        ),
        out_shape=(whole((copies, share, hidden_width), bf16),) * 2,
        compiler_params=pltpu.CompilerParams(vmem_limit_bytes=16 << 20),
        name="token_out",
    )(here, scales, tokens, cotangent, attn_gain[None], *received)
    return (
        pair_next.reshape(rows, width, channels),
        pair_grad.reshape(rows, width, channels),
        bias_weight_grad,
        denoised,
        token_grad,
        weight_grad,
        out_grad,
    )


def solution(mesh):
    return jax.shard_map(
        shards,
        mesh=mesh,
        in_specs=(
            P(("group", "row"), "col", None),
            P(("group", "row"), "col"),
            P(),
            P(),
            P(),
            P(),
            P(),
            P(),
            P(),
            P(),
            P(),
            P(("group", "row"), None, None),
            P(("group", "row")),
            P(),
            P(None, None, "col"),
            P("col", None),
            P(("group", "row"), None, None),
        ),
        out_specs=(
            P(("group", "row"), "col", None),
            P(("group", "row"), "col", None),
            P(),
            P(("group", "row"), "col", None),
            P(("group", "row"), "col", None),
            P(None, ("group", "row"), "col"),
            P("col", ("group", "row")),
        ),
        check_vma=False,
    )
```

profile of v0, /device:TPU:0, one launch (start us, length us, event | category | flops | bytes accessed | tf_op | source)
XLA Modules:
  0.0 99.0 jit_solution(9416392868296522878)
XLA Ops:
  0.7 2.0 %shard_map.216 = bf16[32,2,16,128]{3,2,1,0:T(8,128)(2,1)S(1)} custom-call(bf16[512,128]{1,0:T(8,128)(2,1)} %bitcast.26, s32[16,32]{1,0:T(8,128)} %mask_ref.1, f32[1,128]{1,0:T(1,128)} %bitcast.32, bf16[128,512]{1,0:T(8,128)(2,1)} %proj_ref.1), custom_call_target="tpu_custom_call" | custom-call | tf_op jit(solution)/shard_map/pallas_call | solution.py:791
  2.7 17.4 %all_to_all.25 = bf16[32,32,128]{2,1,0:T(8,128)(2,1)S(1)} all-to-all(bf16[32,32,128]{2,1,0:T(8,128)(2,1)S(1)} %bitcast.20), channel_id=1, replica_groups=mesh['group'=2,'row'=4,'col'=4] {'group','row','col'}, dimensions={0} | all-to-all | bytes 524288 | tf_op jit(solution)/shard_map/all_to_all | solution.py:786
  20.1 1.3 %shard_map.217 = bf16[8,4,16,128]{3,2,1,0:T(8,128)(2,1)} custom-call(bf16[8,4,2,16,128]{4,3,2,1,0:T(8,128)(2,1)S(1)} %bitcast.21), custom_call_target="tpu_custom_call" | custom-call | tf_op jit(solution)/shard_map/pallas_call | solution.py:818
  21.3 2.6 %all-to-all-start.1 = ((bf16[32,16,128]{2,1,0:T(8,128)(2,1)}), bf16[32,16,128]{2,1,0:T(8,128)(2,1)S(1)}, u32[]{:S(2)}, u32[]{:S(2)}) async-start(bf16[32,16,128]{2,1,0:T(8,128)(2,1)} %bitcast.6), calls=%async_computation.1 | async-start | bytes 262144 | tf_op jit(solution)/shard_map/all_to_all | solution.py:786
  23.9 0.1 pad_add_fusion.here_ref
  24.0 8.3 %all-to-all-done.1.in_ref = bf16[32,16,128]{2,1,0:T(8,128)(2,1)S(1)} async-done(((bf16[32,16,128]{2,1,0:T(8,128)(2,1)}), bf16[32,16,128]{2,1,0:T(8,128)(2,1)S(1)}, u32[]{:S(2)}, u32[]{:S(2)}) %all-to-all-start.1) | async-done | bytes 131104 | tf_op jit(solution)/shard_map/all_to_all | solution.py:786
  32.3 3.7 %shard_map.218 = (bf16[512,128]{1,0:T(8,128)(2,1)}, f32[512,128]{1,0:T(8,128)}, bf16[8,4,16,128]{3,2,1,0:T(8,128)(2,1)}) custom-call(s32[2]{0:T(128)S(1)} %pad_add_fusion.here_ref, s32[128]{0:T(128)} %chain_ref.1, bf16[32,16,128]{2,1,0:T(8,128)(2,1)S(1)} %all-to-all-done.1.in_ref, bf16[512,128]{1,0:T(8,128)(2,1)} %bitcast.27, s32[1,128]{1,0:T(1,128)} %bitcast.31, ...), custom_call_target="tpu_custom_call" | custom-call | tf_op jit(solution)/shard_map/pallas_call | solution.py:822
  36.0 2.6 %all-to-all-start.2 = ((bf16[32,16,128]{2,1,0:T(8,128)(2,1)}), bf16[32,16,128]{2,1,0:T(8,128)(2,1)S(1)}, u32[]{:S(2)}, u32[]{:S(2)}) async-start(bf16[32,16,128]{2,1,0:T(8,128)(2,1)} %bitcast.13), calls=%async_computation.2 | async-start | bytes 262144 | tf_op jit(solution)/shard_map/all_to_all | solution.py:786
  38.6 0.6 broadcast_in_dim.26.gain_ref
  39.2 5.1 %shard_map.219 = (bf16[384,192]{1,0:T(8,128)(2,1)}, bf16[384,192]{1,0:T(8,128)(2,1)}, bf16[384,192]{1,0:T(8,128)(2,1)}, bf16[384,192]{1,0:T(8,128)(2,1)}, f32[38...) custom-call(f32[3]{0:T(128)S(1)} %add_rsqrt_fusion.scale_ref, ...), custom_call_target="tpu_custom_call" | custom-call | tf_op jit(solution)/shard_map/pallas_call | solution.py:802
  44.3 2.6 %all-to-all-done.2 = bf16[32,16,128]{2,1,0:T(8,128)(2,1)S(1)} async-done(((bf16[32,16,128]{2,1,0:T(8,128)(2,1)}), bf16[32,16,128]{2,1,0:T(8,128)(2,1)S(1)}, u32[]{:S(2)}, u32[]{:S(2)}) %all-to-all-start.2) | async-done | bytes 131104 | tf_op jit(solution)/shard_map/all_to_all | solution.py:786
  46.9 6.3 %shard_map.220 = (bf16[8,4,16,128]{3,2,1,0:T(8,128)(2,1)}, bf16[384,192]{1,0:T(8,128)(2,1)}, bf16[4,384,192]{2,1,0:T(8,128)(2,1)}, bf16[2,3,32,768]{3,2,1,0:T(8,...) custom-call(s32[2]{0:T(128)S(1)} %pad_add_fusion.here_ref, ...), custom_call_target="tpu_custom_call" | custom-call | tf_op jit(solution)/shard_map/pallas_call | solution.py:855
  53.2 4.3 %shard_map.222 = (bf16[4,96,1024]{2,1,0:T(8,128)(2,1)}, bf16[4,96,1024]{2,1,0:T(8,128)(2,1)}) custom-call(s32[2]{0:T(128)S(1)} %pad_add_fusion.here_ref, bf16[768,384]{1,0:T(8,128)(2,1)} %get-tuple-element.59.hidden_t_ref, bf16[768,384]{1,0:T(8,128)(2,1)} %get-tuple-element.60.cot_t_ref, bf16[4,384,192]{2,1,0:T(8,128)(2,1)} %get-tuple-element.61.grads_ref, ...), custom_call_target="tpu_custom_call" | custom-call | tf_op jit(solution)/shard_map/pallas_call | solution.py:895
  57.5 3.3 %all-to-all-start.3 = ((bf16[32,16,128]{2,1,0:T(8,128)(2,1)}), bf16[32,16,128]{2,1,0:T(8,128)(2,1)S(1)}, u32[]{:S(2)}, u32[]{:S(2)}) async-start(bf16[32,16,128]{2,1,0:T(8,128)(2,1)} %bitcast.16), calls=%async_computation.3 | async-start | bytes 262144 | tf_op jit(solution)/shard_map/all_to_all | solution.py:786
  60.8 0.0 copy-start
  60.8 0.0 copy-start.1
  60.9 0.0 copy-start.3
  60.9 1.8 %collective-permute-start = (bf16[2,3,32,768]{3,2,1,0:T(8,128)(2,1)}, bf16[2,3,32,768]{3,2,1,0:T(8,128)(2,1)S(1)}, u32[]{:S(2)}, u32[]{:S(2)}) collective-permute-start(bf16[2,3,32,768]{3,2,1,0:T(8,128)(2,1)} %get-tuple-element.54), channel_id=1, source_target_pairs={{0,1},{1,2},{2,3},{3,0},{4,5},{5,6},{6,7},{7,4},{8,9},{9,10},{10,1... | collective-permute-start | bytes 884744 | tf_op jit(solution)/shard_map/ppermute | solution.py:789
  62.7 2.4 %collective-permute-start.1 = (bf16[2,3,32,768]{3,2,1,0:T(8,128)(2,1)}, bf16[2,3,32,768]{3,2,1,0:T(8,128)(2,1)S(1)}, u32[]{:S(2)}, u32[]{:S(2)}) collective-permute-start(bf16[2,3,32,768]{3,2,1,0:T(8,128)(2,1)} %get-tuple-element.55), channel_id=1, source_target_pairs={{0,2},{1,3},{2,0},{3,1},{4,6},{5,7},{6,4},{7,5},{8,10},{9,11},{10,... | collective-permute-start | bytes 884744 | tf_op jit(solution)/shard_map/ppermute | solution.py:789
  65.1 1.4 %collective-permute-start.2 = (bf16[2,3,32,768]{3,2,1,0:T(8,128)(2,1)}, bf16[2,3,32,768]{3,2,1,0:T(8,128)(2,1)S(1)}, u32[]{:S(2)}, u32[]{:S(2)}) collective-permute-start(bf16[2,3,32,768]{3,2,1,0:T(8,128)(2,1)} %get-tuple-element.56), channel_id=1, source_target_pairs={{0,3},{1,0},{2,1},{3,2},{4,7},{5,4},{6,5},{7,6},{8,11},{9,8},{10,9... | collective-permute-start | bytes 884744 | tf_op jit(solution)/shard_map/ppermute | solution.py:789
  66.5 3.1 %all-to-all-done.3 = bf16[32,16,128]{2,1,0:T(8,128)(2,1)S(1)} async-done(((bf16[32,16,128]{2,1,0:T(8,128)(2,1)}), bf16[32,16,128]{2,1,0:T(8,128)(2,1)S(1)}, u32[]{:S(2)}, u32[]{:S(2)}) %all-to-all-start.3) | async-done | bytes 131104 | tf_op jit(solution)/shard_map/all_to_all | solution.py:786
  69.6 3.0 %shard_map.221 = (f32[512,128]{1,0:T(8,128)}, bf16[32,16,128]{2,1,0:T(8,128)(2,1)}) custom-call(bf16[8,4,16,128]{3,2,1,0:T(8,128)(2,1)S(1)} %bitcast.23, f32[512,128]{1,0:T(8,128)} %get-tuple-element.50.updated_ref, f32[1,128]{1,0:T(1,128)} %bitcast.35, bf16[16,128]{1,0:T(8,128)(2,1)} %bitcast.29), custom_call_target="tpu_custom_call" | custom-call | tf_op jit(solution)/shard_map/pallas_call | solution.py:919
  72.6 2.6 %all-to-all-start.4 = ((bf16[32,16,128]{2,1,0:T(8,128)(2,1)}), bf16[32,16,128]{2,1,0:T(8,128)(2,1)S(1)}, u32[]{:S(2)}, u32[]{:S(2)}) async-start(bf16[32,16,128]{2,1,0:T(8,128)(2,1)} %get-tuple-element.52), calls=%async_computation.4 | async-start | bytes 262144 | tf_op jit(solution)/shard_map/all_to_all | solution.py:786
  75.2 2.5 %shard_map.223 = (bf16[96,1024]{1,0:T(8,128)(2,1)}, bf16[96,1024]{1,0:T(8,128)(2,1)}, bf16[96,1024]{1,0:T(8,128)(2,1)}, bf16[96,1024]{1,0:T(8,128)(2,1)}) custom-call(s32[2]{0:T(128)S(1)} %pad_add_fusion.here_ref, bf16[4,96,1024]{2,1,0:T(8,128)(2,1)} %get-tuple-element.63.keep_ref, bf16[4,96,1024]{2,1,0:T(8,128)(2,1)S(1)} %collective-permute-done.3.got_ref), custom_call_target="tpu_custom_call" | custom-call | tf_op jit(solution)/shard_map/pallas_call | solution.py:904
  77.6 1.7 %collective-permute-start.4 = (bf16[96,1024]{1,0:T(8,128)(2,1)}, bf16[96,1024]{1,0:T(8,128)(2,1)S(1)}, u32[]{:S(2)}, u32[]{:S(2)}) collective-permute-start(bf16[96,1024]{1,0:T(8,128)(2,1)} %get-tuple-element.66), channel_id=1, source_target_pairs={{0,8},{4,12},{8,0},{12,4},{16,24},{20,28},{24,16},{28,20},{1,9},{5... | collective-permute-start | bytes 589832 | tf_op jit(solution)/shard_map/ppermute | solution.py:915
  79.3 1.5 %collective-permute-start.5 = (bf16[96,1024]{1,0:T(8,128)(2,1)}, bf16[96,1024]{1,0:T(8,128)(2,1)S(1)}, u32[]{:S(2)}, u32[]{:S(2)}) collective-permute-start(bf16[96,1024]{1,0:T(8,128)(2,1)} %get-tuple-element.67), channel_id=1, source_target_pairs={{0,16},{4,20},{8,24},{12,28},{16,0},{20,4},{24,8},{28,12},{1,17},{... | collective-permute-start | bytes 589832 | tf_op jit(solution)/shard_map/ppermute | solution.py:915
  80.7 0.4 collective-permute-start.6
  81.1 5.8 %collective-permute-done.1.refs_2_ = bf16[2,3,32,768]{3,2,1,0:T(8,128)(2,1)S(1)} collective-permute-done((bf16[2,3,32,768]{3,2,1,0:T(8,128)(2,1)}, bf16[2,3,32,768]{3,2,1,0:T(8,128)(2,1)S(1)}, u32[]{:S(2)}, u32[]{:S(2)}) %collective-permute-start.1) | collective-permute-done | bytes 294944 | tf_op jit(solution)/shard_map/ppermute | solution.py:789
  86.9 2.1 %token_out.1 = (bf16[3,32,768]{2,1,0:T(8,128)(2,1)}, bf16[3,32,768]{2,1,0:T(8,128)(2,1)}) custom-call(s32[2]{0:T(128)S(1)} %pad_add_fusion.here_ref, f32[3]{0:T(128)S(1)} %add_rsqrt_fusion.scale_ref, bf16[3,128,768]{2,1,0:T(8,128)(2,1)S(1)} %copy-done, bf16[3,128,768]{2,1,0:T(8,128)(2,1)S(1)} %copy-done.1, f32[1,768]{1,0:T(1,128)S(1)} %copy-done.3, ...), custom_call_target="tpu_custom_call" | custom-call | tf_op jit(solution)/shard_map/token_out/pallas_call | solution.py:945
  89.1 7.4 %all-to-all-done.4 = bf16[32,16,128]{2,1,0:T(8,128)(2,1)S(1)} async-done(((bf16[32,16,128]{2,1,0:T(8,128)(2,1)}), bf16[32,16,128]{2,1,0:T(8,128)(2,1)S(1)}, u32[]{:S(2)}, u32[]{:S(2)}) %all-to-all-start.4) | async-done | bytes 131104 | tf_op jit(solution)/shard_map/all_to_all | solution.py:786
  96.5 0.6 convert_reduce_fusion
  97.1 1.8 %shard_map.224 = (f32[4,96,192]{2,1,0:T(8,128)}, f32[192,96]{1,0:T(8,128)}) custom-call(bf16[96,1024]{1,0:T(8,128)(2,1)} %get-tuple-element.65.refs_0_, bf16[96,1024]{1,0:T(8,128)(2,1)S(1)} %collective-permute-done.4.refs_1_, bf16[96,1024]{1,0:T(8,128)(2,1)S(1)} %collective-permute-done.5.refs_2_, bf16[96,1024]{1,0:T(8,128)(2,1)S(1)} %collective-permute-done.6.refs_3_), custom_call_target="tpu_custom_call" | custom-call | tf_op jit(solution)/shard_map/pallas_call | solution.py:932
  (17 shorter events, 0.0 us)
Async XLA Ops:
  0.6 37.9 %copy-start.4 = (f32[768]{0:T(1024)S(1)}, f32[768]{0:T(1024)}, u32[]{:S(2)}) copy-start(f32[768]{0:T(1024)} %param.30) | copy-start | bytes 9220
  0.6 38.5 %copy-start.5 = (s32[3]{0:T(128)S(1)}, s32[3]{0:T(128)}, u32[]{:S(2)}) copy-start(s32[3]{0:T(128)} %param.29) | copy-start | bytes 40
  21.3 11.0 %all-to-all-start.1 = ((bf16[32,16,128]{2,1,0:T(8,128)(2,1)}), bf16[32,16,128]{2,1,0:T(8,128)(2,1)S(1)}, u32[]{:S(2)}, u32[]{:S(2)}) async-start(bf16[32,16,128]{2,1,0:T(8,128)(2,1)} %bitcast.6), calls=%async_computation.1 | async-start | bytes 262144 | tf_op jit(solution)/shard_map/all_to_all | solution.py:786
  36.0 11.0 %all-to-all-start.2 = ((bf16[32,16,128]{2,1,0:T(8,128)(2,1)}), bf16[32,16,128]{2,1,0:T(8,128)(2,1)S(1)}, u32[]{:S(2)}, u32[]{:S(2)}) async-start(bf16[32,16,128]{2,1,0:T(8,128)(2,1)} %bitcast.13), calls=%async_computation.2 | async-start | bytes 262144 | tf_op jit(solution)/shard_map/all_to_all | solution.py:786
  57.5 17.7 %collective-permute-start.3 = (bf16[4,96,1024]{2,1,0:T(8,128)(2,1)}, bf16[4,96,1024]{2,1,0:T(8,128)(2,1)S(1)}, u32[]{:S(2)}, u32[]{:S(2)}) collective-permute-start(bf16[4,96,1024]{2,1,0:T(8,128)(2,1)} %get-tuple-element.64), channel_id=1, source_target_pairs={{0,4},{4,0},{8,12},{12,8},{16,20},{20,16},{24,28},{28,24},{1,5},{5... | collective-permute-start | bytes 2359304 | tf_op jit(solution)/shard_map/ppermute | solution.py:903
  57.5 12.1 %all-to-all-start.3 = ((bf16[32,16,128]{2,1,0:T(8,128)(2,1)}), bf16[32,16,128]{2,1,0:T(8,128)(2,1)S(1)}, u32[]{:S(2)}, u32[]{:S(2)}) async-start(bf16[32,16,128]{2,1,0:T(8,128)(2,1)} %bitcast.16), calls=%async_computation.3 | async-start | bytes 262144 | tf_op jit(solution)/shard_map/all_to_all | solution.py:786
  60.8 26.1 %copy-start = (bf16[3,128,768]{2,1,0:T(8,128)(2,1)S(1)}, bf16[3,128,768]{2,1,0:T(8,128)(2,1)}, u32[]{:S(2)}) copy-start(bf16[3,128,768]{2,1,0:T(8,128)(2,1)} %tokens_ref.3) | copy-start | bytes 1769476
  60.8 26.1 %copy-start.1 = (bf16[3,128,768]{2,1,0:T(8,128)(2,1)S(1)}, bf16[3,128,768]{2,1,0:T(8,128)(2,1)}, u32[]{:S(2)}) copy-start(bf16[3,128,768]{2,1,0:T(8,128)(2,1)} %cot_ref.3) | copy-start | bytes 1769476
  60.8 26.0 %copy-start.2 = (bf16[2,3,32,768]{3,2,1,0:T(8,128)(2,1)S(1)}, bf16[2,3,32,768]{3,2,1,0:T(8,128)(2,1)}, u32[]{:S(2)}) copy-start(bf16[2,3,32,768]{3,2,1,0:T(8,128)(2,1)} %get-tuple-element.53.refs_0_) | copy-start | bytes 884740
  60.9 26.0 %copy-start.3 = (f32[1,768]{1,0:T(1,128)S(1)}, f32[1,768]{1,0:T(1,128)}, u32[]{:S(2)}) copy-start(f32[1,768]{1,0:T(1,128)} %broadcast_in_dim.26.gain_ref) | copy-start | bytes 9220
  60.9 19.9 %collective-permute-start = (bf16[2,3,32,768]{3,2,1,0:T(8,128)(2,1)}, bf16[2,3,32,768]{3,2,1,0:T(8,128)(2,1)S(1)}, u32[]{:S(2)}, u32[]{:S(2)}) collective-permute-start(bf16[2,3,32,768]{3,2,1,0:T(8,128)(2,1)} %get-tuple-element.54), channel_id=1, source_target_pairs={{0,1},{1,2},{2,3},{3,0},{4,5},{5,6},{6,7},{7,4},{8,9},{9,10},{10,1... | collective-permute-start | bytes 884744 | tf_op jit(solution)/shard_map/ppermute | solution.py:789
  62.7 24.2 %collective-permute-start.1 = (bf16[2,3,32,768]{3,2,1,0:T(8,128)(2,1)}, bf16[2,3,32,768]{3,2,1,0:T(8,128)(2,1)S(1)}, u32[]{:S(2)}, u32[]{:S(2)}) collective-permute-start(bf16[2,3,32,768]{3,2,1,0:T(8,128)(2,1)} %get-tuple-element.55), channel_id=1, source_target_pairs={{0,2},{1,3},{2,0},{3,1},{4,6},{5,7},{6,4},{7,5},{8,10},{9,11},{10,... | collective-permute-start | bytes 884744 | tf_op jit(solution)/shard_map/ppermute | solution.py:789
  65.1 21.8 %collective-permute-start.2 = (bf16[2,3,32,768]{3,2,1,0:T(8,128)(2,1)}, bf16[2,3,32,768]{3,2,1,0:T(8,128)(2,1)S(1)}, u32[]{:S(2)}, u32[]{:S(2)}) collective-permute-start(bf16[2,3,32,768]{3,2,1,0:T(8,128)(2,1)} %get-tuple-element.56), channel_id=1, source_target_pairs={{0,3},{1,0},{2,1},{3,2},{4,7},{5,4},{6,5},{7,6},{8,11},{9,8},{10,9... | collective-permute-start | bytes 884744 | tf_op jit(solution)/shard_map/ppermute | solution.py:789
  72.6 23.9 %all-to-all-start.4 = ((bf16[32,16,128]{2,1,0:T(8,128)(2,1)}), bf16[32,16,128]{2,1,0:T(8,128)(2,1)S(1)}, u32[]{:S(2)}, u32[]{:S(2)}) async-start(bf16[32,16,128]{2,1,0:T(8,128)(2,1)} %get-tuple-element.52), calls=%async_computation.4 | async-start | bytes 262144 | tf_op jit(solution)/shard_map/all_to_all | solution.py:786
  77.6 19.5 %collective-permute-start.4 = (bf16[96,1024]{1,0:T(8,128)(2,1)}, bf16[96,1024]{1,0:T(8,128)(2,1)S(1)}, u32[]{:S(2)}, u32[]{:S(2)}) collective-permute-start(bf16[96,1024]{1,0:T(8,128)(2,1)} %get-tuple-element.66), channel_id=1, source_target_pairs={{0,8},{4,12},{8,0},{12,4},{16,24},{20,28},{24,16},{28,20},{1,9},{5... | collective-permute-start | bytes 589832 | tf_op jit(solution)/shard_map/ppermute | solution.py:915
  79.3 17.8 %collective-permute-start.5 = (bf16[96,1024]{1,0:T(8,128)(2,1)}, bf16[96,1024]{1,0:T(8,128)(2,1)S(1)}, u32[]{:S(2)}, u32[]{:S(2)}) collective-permute-start(bf16[96,1024]{1,0:T(8,128)(2,1)} %get-tuple-element.67), channel_id=1, source_target_pairs={{0,16},{4,20},{8,24},{12,28},{16,0},{20,4},{24,8},{28,12},{1,17},{... | collective-permute-start | bytes 589832 | tf_op jit(solution)/shard_map/ppermute | solution.py:915
  80.7 16.4 %collective-permute-start.6 = (bf16[96,1024]{1,0:T(8,128)(2,1)}, bf16[96,1024]{1,0:T(8,128)(2,1)S(1)}, u32[]{:S(2)}, u32[]{:S(2)}) collective-permute-start(bf16[96,1024]{1,0:T(8,128)(2,1)} %get-tuple-element.68), channel_id=1, source_target_pairs={{0,24},{4,28},{8,16},{12,20},{16,8},{20,12},{24,0},{28,4},{1,25},{... | collective-permute-start | bytes 589832 | tf_op jit(solution)/shard_map/ppermute | solution.py:915
where the time goes:
time: 99.5 us; the launch traced here: 99 us
  Pallas kernels  32 us (32%)
  waiting for transfers between devices  27.2 us (27%)
  starting transfers between devices  20.2 us (20%)
  blocking collectives  17.4 us (17%)
    all_to_all x4, waiting for transfers between devices, exchange(): return lax.all_to_all(values, axes, 0, 0, tiled=True)  21.4 us
    all_to_all x1, blocking collectives, exchange(): return lax.all_to_all(values, axes, 0, 0, tiled=True)  17.4 us
    all_to_all x4, starting transfers between devices, exchange(): return lax.all_to_all(values, axes, 0, 0, tiled=True)  11.1 us
    pallas_call x1, Pallas kernels, shards(): call(attention_kernel, 20, (whole((stripes, cols, rows, LANES), bf16), pl...  6.26 us
    ppermute x3, waiting for transfers between devices, shift(): lax.ppermute(values, 'col', [(i, (i + k) % cols) for i in range(cols)])  5.78 us
    ppermute x3, starting transfers between devices, shift(): lax.ppermute(values, 'col', [(i, (i + k) % cols) for i in range(cols)])  5.65 us
    pallas_call x1, Pallas kernels, shards(): call(token_in_kernel, 16, (*[pltpu.HBM((tall, inner), bf16)] * 4, *[pltpu...  5.13 us
    pallas_call x1, Pallas kernels, shards(): call(weight_in_kernel, 16, (pltpu.HBM((chips, block, 8 * LANES), bf16),)...  4.29 us
  transfers between devices with their start and end apart: 11, of which 5 were waited for; matrix products, arithmetic and copies ran while one was open for 1% of the time, Pallas kernels for 13%

commit v1 on v0

--- a/solution.py
+++ b/solution.py
@@ -289,6 +289,10 @@
 
 def far(values):
     return pltpu.with_memory_space_constraint(values, pltpu.HBM)
+
+
+def near(values):
+    return pltpu.with_memory_space_constraint(values, pltpu.VMEM)
 
 
 def pair_in_kernel(pair_ref, mask_ref, gain_ref, proj_ref, out_ref, rows_ref):
@@ -515,7 +519,6 @@
     score_ref,
     prob_ref,
     weight_ref,
-    out_weight_ref,
     pair_ref,
     outs_ref,
     grads_ref,
@@ -526,7 +529,7 @@
     part_refs, (sums_ref, parts_ref) = refs[:-2], refs[-2:]
     stripes, cols, rows, _ = bias_ref.shape
     copies, heads, length, _ = score_ref.shape
-    inner, hidden_width = out_weight_ref.shape
+    inner, hidden_width = weight_ref.shape[1:]
     share = length // cols
     lanes = lane_groups(length, width)
     head_of = lax.broadcasted_iota(jnp.int32, (length, inner), 1) // head_size
@@ -574,12 +577,19 @@
         outs_ref[part] = gated_out
         for g in range(4):
             grads_ref[g, part] = grads[g]
-        out_part = dot_nn(gated_out, out_weight_ref[...])
         in_part = dot_nn(grads[0], weight_ref[0])
         for g in range(1, 4):
             in_part += dot_nn(grads[g], weight_ref[g])
-        parts_ref[:, 0, t] = out_part.astype(jnp.bfloat16).reshape(cols, share, hidden_width)
-        parts_ref[:, 1, t] = in_part.astype(jnp.bfloat16).reshape(cols, share, hidden_width)
+        tail = jnp.concatenate(
+            [gated_out[:, LANES:], jnp.zeros((length, 2 * LANES - inner), jnp.bfloat16)], axis=1
+        )
+        for first, values in (
+            (0, in_part.astype(jnp.bfloat16)),
+            (hidden_width, gated_out[:, :LANES]),
+            (hidden_width + LANES, tail),
+        ):
+            size = values.shape[1]
+            parts_ref[:, t, :, first : first + size] = values.reshape(cols, share, size)
     for k in range(cols):
         part_refs[k][...] = parts_ref[(here_ref[1] + k) % cols]
     for col in range(cols):
@@ -631,7 +641,9 @@
     heads = bias_weight_ref.shape[0]
     groups = LANES // width
     total = jnp.sum(in_ref[...].astype(jnp.float32), 0).reshape(cols * rows, LANES)
-    spread = dot_tn(head_gather(rows, cols, heads), total, precision=lax.Precision.HIGHEST)
+    spread = dot_tn(
+        head_gather(rows, cols, heads).astype(jnp.bfloat16), total.astype(jnp.bfloat16)
+    )
     lanes = lane_groups(heads, width)
     head_group = lax.broadcasted_iota(jnp.int32, (heads, LANES), 0) % groups
     blocks = []
@@ -645,33 +657,44 @@
                 turned = jnp.where(head_group == g, turn(tile, s - g, width), turned)
             tiles.append(turned)
         blocks.append(merge(tiles, lanes))
-    grad_t = jnp.concatenate(blocks, axis=1)
+    grad_t = jnp.concatenate(blocks, axis=1).astype(jnp.bfloat16)
     updated = updated_ref[...]
     gain = gain_ref[...]
-    grad_in = lax.dot_general(
-        grad_t,
-        bias_weight_ref[...].astype(jnp.float32),
-        (((0,), (0,)), ((), ())),
-        precision=lax.Precision.HIGHEST,
-        preferred_element_type=jnp.float32,
-    )
+    grad_in = dot_tn(grad_t, bias_weight_ref[...])
     grad_ref[...] = norm_back(grad_in, updated, gain)
-    bias_in = (normalize(updated) * gain).astype(jnp.bfloat16).astype(jnp.float32)
-    weight = dot_nn(grad_t, bias_in, precision=lax.Precision.HIGHEST).astype(jnp.bfloat16)
+    bias_in = (normalize(updated) * gain).astype(jnp.bfloat16)
+    weight = dot_nn(grad_t, bias_in).astype(jnp.bfloat16)
     for device in range(weight_ref.shape[0]):
         weight_ref[device] = weight
 
 
-def token_out_kernel(here_ref, scale_ref, tokens_ref, cot_ref, gain_ref, *refs):
-    part_refs, (out_ref, grad_ref) = refs[:-2], refs[-2:]
-    for t in range(out_ref.shape[0]):
-        sums = part_refs[0][:, t].astype(jnp.float32)
-        for r in part_refs[1:]:
-            sums = sums + r[:, t].astype(jnp.float32)
+def token_out_kernel(here_ref, scale_ref, tokens_ref, cot_ref, gain_ref, weight_ref, *refs):
+    out_ref, grad_ref, halves_ref, sums_ref = refs[-4:]
+    copies, share, hidden_width = out_ref.shape
+    inner = weight_ref.shape[0]
+    others = halves_ref.shape[0]
+    part_refs, mine_refs, other_refs = (
+        refs[: others + 1],
+        refs[others + 1 : 2 * others + 1],
+        refs[2 * others + 1 : 3 * others + 1],
+    )
+    core = here_ref[0] % 2
+    for k in range(others):
+        halves_ref[k, core] = mine_refs[k][...]
+        halves_ref[k, 1 - core] = other_refs[k][...]
+    for k in range(others + 1):
+        gated = part_refs[k][:, :, hidden_width : hidden_width + inner]
+        weight = weight_ref[...] if k == 0 else halves_ref[k - 1].reshape(inner, hidden_width)
+        product = dot_nn(gated.reshape(copies * share, inner), weight)
+        sums_ref[...] = product if k == 0 else sums_ref[...] + product
+    for t in range(copies):
+        grad_hidden = part_refs[0][t, :, :hidden_width].astype(jnp.float32)
+        for r in part_refs[1 : others + 1]:
+            grad_hidden = grad_hidden + r[t, :, :hidden_width].astype(jnp.float32)
         scale = scale_ref[t]
         scaled = scale * tokens_ref[t].astype(jnp.float32)
-        out_ref[t] = (scaled + sums[0]).astype(jnp.bfloat16)
-        grad = cot_ref[t].astype(jnp.float32) + norm_back(sums[1], scaled, gain_ref[...])
+        out_ref[t] = (scaled + sums_ref[t * share : (t + 1) * share]).astype(jnp.bfloat16)
+        grad = cot_ref[t].astype(jnp.float32) + norm_back(grad_hidden, scaled, gain_ref[...])
         grad_ref[t] = (scale * grad).astype(jnp.bfloat16)
 
 
@@ -797,15 +820,17 @@
         [pltpu.VMEM((devices * rows, LANES), f32)],
     )(far(pair_flat), far(pair_mask), far(tri_in_gain[None]), far(tri_proj))
     sides = exchange(projected.reshape(devices, 2 * rows, LANES), all_axes)
+    half = lax.dynamic_slice_in_dim(out_weight, row_index % 2 * (inner // 2), inner // 2, 0)
+    halves = [shift(half, k) for k in range(1, cols)]
     tall = copies * length
     local = heads_all // cols
     query, key_rows, value, gated, gate_sig, grad_gated, scores, probs, hidden_t, cot_t = call(
         token_in_kernel,
         16,
         (
-            *[pltpu.HBM((tall, inner), bf16)] * 4,
-            *[pltpu.HBM((tall, inner), f32)] * 2,
-            *[pltpu.HBM((copies, local, length, length), f32)] * 2,
+            *[pltpu.VMEM((tall, inner), bf16)] * 4,
+            *[pltpu.VMEM((tall, inner), f32)] * 2,
+            *[pltpu.VMEM((copies, local, length, length), f32)] * 2,
             *[pltpu.HBM((hidden_width, tall), bf16)] * 2,
         ),
         1,
@@ -851,21 +876,22 @@
         ),
     )
     head_bias = exchange(bias_tile.reshape(devices, rows, LANES), all_axes)
-    part = pltpu.HBM((2, copies, length // cols, hidden_width), bf16)
+    share = length // cols
+    part = pltpu.HBM((copies, share, hidden_width + 2 * LANES), bf16)
     bias_sums, outs, grads, *parts = call(
         attention_kernel,
         20,
         (
-            whole((stripes, cols, rows, LANES), bf16),
+            pltpu.HBM((stripes, cols, rows, LANES), bf16),
             pltpu.HBM((tall, inner), bf16),
             pltpu.HBM((4, tall, inner), bf16),
             *[part] * cols,
         ),
         1,
-        11,
+        10,
         [
             pltpu.VMEM((local, length, length), f32),
-            pltpu.VMEM((cols, 2, copies, length // cols, hidden_width), bf16),
+            pltpu.VMEM((cols, copies, share, hidden_width + 2 * LANES), bf16),
         ],
         width=width,
         head_size=head_size,
@@ -873,29 +899,24 @@
         here,
         head_bias.reshape(stripes, cols, rows, LANES),
         *map(
-            far,
-            (
-                query,
-                key_rows,
-                value,
-                gated,
-                gate_sig,
-                grad_gated,
-                scores,
-                probs,
-                weight_t,
-                out_weight,
-            ),
+            near,
+            (query, key_rows, value, gated, gate_sig, grad_gated, scores, probs),
         ),
+        far(weight_t),
     )
     bias_back = exchange(bias_sums.reshape(devices, rows, LANES), all_axes)
     received = [parts[0]] + [shift(parts[k], k) for k in range(1, cols)]
+    others = []
+    for k in range(1, cols):
+        others.append(
+            lax.ppermute(halves[k - 1], stripe_axes, [(i, i ^ 1) for i in range(stripes)])
+        )
     chips = stripes // 2
     block = hidden_width // stripes
     keep, give = call(
         weight_in_kernel,
         16,
-        (pltpu.HBM((chips, block, 8 * LANES), bf16),) * 2,
+        (pltpu.VMEM((chips, block, 8 * LANES), bf16),) * 2,
         1,
         4,
         [pltpu.VMEM((chips, 2, block, 8 * LANES), bf16)],
@@ -904,11 +925,14 @@
     mine, *give = call(
         weight_add_kernel,
         12,
-        (pltpu.HBM((block, 8 * LANES), bf16),) * chips,
+        (
+            pltpu.HBM((block, 8 * LANES), bf16),
+            *[pltpu.VMEM((block, 8 * LANES), bf16)] * (chips - 1),
+        ),
         1,
         2,
         [pltpu.VMEM((chips, block, 8 * LANES), bf16)],
-    )(here, far(keep), got)
+    )(here, near(keep), near(got))
     wires = [mine]
     for k in range(1, chips):
         wires.append(
@@ -938,8 +962,7 @@
         ),
         0,
         chips,
-    )(far(wires[0]), *wires[1:])
-    share = length // cols
+    )(far(wires[0]), *map(near, wires[1:]))
     mine = pl.BlockSpec((copies, share, hidden_width), lambda i, here: (0, here[1], 0))
     fixed = lambda shape: pl.BlockSpec(shape, lambda i, here: (0,) * len(shape))
     denoised, token_grad = pl.pallas_call(
@@ -947,13 +970,29 @@
         grid_spec=pltpu.PrefetchScalarGridSpec(
             num_scalar_prefetch=1,
             grid=(1,),
-            in_specs=[smem, mine, mine, fixed((1, hidden_width))] + [fixed((2, copies, share, hidden_width))] * cols,
+            in_specs=[smem, mine, mine, fixed((1, hidden_width)), fixed((inner, hidden_width))]
+            + [fixed((copies, share, hidden_width + 2 * LANES))] * cols
+            + [fixed((inner // 2, hidden_width))] * (2 * cols - 2),
             out_specs=[fixed((copies, share, hidden_width))] * 2,
+            scratch_shapes=[
+                pltpu.VMEM((cols - 1, 2, inner // 2, hidden_width), bf16),
+                pltpu.VMEM((copies * share, hidden_width), f32),
+            ],
         ),
         out_shape=(whole((copies, share, hidden_width), bf16),) * 2,
         compiler_params=pltpu.CompilerParams(vmem_limit_bytes=16 << 20),
         name="token_out",
-    )(here, scales, tokens, cotangent, attn_gain[None], *received)
+    )(
+        here,
+        scales,
+        tokens,
+        cotangent,
+        attn_gain[None],
+        out_weight,
+        *received,
+        *halves,
+        *others,
+    )
     return (
         pair_next.reshape(rows, width, channels),
         pair_grad.reshape(rows, width, channels),

time: 99.5 us -> 104 us (1.045); the launches traced: 99 us -> 102 us
  starting transfers between devices: 20.2 us -> 30.8 us
  waiting for transfers between devices: 27.2 us -> 21.2 us
  Pallas kernels: 32 us -> 29.3 us
  local copies, waits for them, and re-layouts: 0.61 us -> 1.93 us
    all_to_all x4, waiting for transfers between devices: 21.4 us -> 11.5 us  [exchange(): return lax.all_to_all(values, axes, 0, 0, tiled=True)]
    ppermute x3 -> x6, starting transfers between devices: 5.65 us -> 14 us  [shift(): lax.ppermute(values, 'col', [(i, (i + k) % cols) for i in range(cols)])]
    ppermute x3 -> x6, waiting for transfers between devices: 5.78 us -> 9.7 us  [shift(): lax.ppermute(values, 'col', [(i, (i + k) % cols) for i in range(cols)])]
    pallas_call x4, Pallas kernels: 18.1 us -> 15.2 us  [the longest x1 4.73 us: shards(): call(attention_kernel, 20, (pltpu.HBM((stripes, cols, rows, LANES), bf16)...]
    all_to_all x4, starting transfers between devices: 11.1 us -> 12.8 us  [exchange(): return lax.all_to_all(values, axes, 0, 0, tiled=True)]
  transfers between devices with their start and end apart: 11 -> 17, of which waited for: 5 -> 4; matrix products, arithmetic and copies ran while one was open for 1% -> 2% of each run, Pallas kernels for 13% -> 12%
where the time goes in v1:
time: 104 us; the launch traced here: 102 us
  starting transfers between devices  30.8 us (30%)
  Pallas kernels  29.3 us (28%)
  waiting for transfers between devices  21.2 us (20%)
  blocking collectives  17.4 us (17%)
  local copies, waits for them, and re-layouts  1.93 us (2%)
    all_to_all x1, blocking collectives, exchange(): return lax.all_to_all(values, axes, 0, 0, tiled=True)  17.4 us
    ppermute x6, starting transfers between devices, shift(): lax.ppermute(values, 'col', [(i, (i + k) % cols) for i in range(cols)])  14 us
    all_to_all x4, starting transfers between devices, exchange(): return lax.all_to_all(values, axes, 0, 0, tiled=True)  12.8 us
    all_to_all x4, waiting for transfers between devices, exchange(): return lax.all_to_all(values, axes, 0, 0, tiled=True)  11.5 us
    ppermute x6, waiting for transfers between devices, shift(): lax.ppermute(values, 'col', [(i, (i + k) % cols) for i in range(cols)])  9.7 us
    pallas_call x1, Pallas kernels, shards(): call(attention_kernel, 20, (pltpu.HBM((stripes, cols, rows, LANES), bf16)...  4.73 us
    pallas_call x1, Pallas kernels, shards(): call(token_in_kernel, 16, (*[pltpu.VMEM((tall, inner), bf16)] * 4, *[pltp...  4.6 us
    pallas_call x1, Pallas kernels, shards(): call(weight_in_kernel, 16, (pltpu.VMEM((chips, block, 8 * LANES), bf16),)...  4.04 us
  transfers between devices with their start and end apart: 17, of which 4 were waited for; matrix products, arithmetic and copies ran while one was open for 2% of the time, Pallas kernels for 12%

profile of v1, /device:TPU:0, one launch (start us, length us, event | category | flops | bytes accessed | tf_op | source)
XLA Modules:
  0.0 102.1 jit_solution(8002044564657657858)
XLA Ops:
  0.7 2.0 %shard_map.216 = bf16[32,2,16,128]{3,2,1,0:T(8,128)(2,1)S(1)} custom-call(bf16[512,128]{1,0:T(8,128)(2,1)} %bitcast.26, s32[16,32]{1,0:T(8,128)} %mask_ref.1, f32[1,128]{1,0:T(1,128)} %bitcast.32, bf16[128,512]{1,0:T(8,128)(2,1)} %proj_ref.1), custom_call_target="tpu_custom_call" | custom-call | tf_op jit(solution)/shard_map/pallas_call | solution.py:814
  2.7 17.4 %all_to_all.25 = bf16[32,32,128]{2,1,0:T(8,128)(2,1)S(1)} all-to-all(bf16[32,32,128]{2,1,0:T(8,128)(2,1)S(1)} %bitcast.20), channel_id=1, replica_groups=mesh['group'=2,'row'=4,'col'=4] {'group','row','col'}, dimensions={0} | all-to-all | bytes 524288 | tf_op jit(solution)/shard_map/all_to_all | solution.py:809
  20.1 1.3 %shard_map.217 = bf16[8,4,16,128]{3,2,1,0:T(8,128)(2,1)} custom-call(bf16[8,4,2,16,128]{4,3,2,1,0:T(8,128)(2,1)S(1)} %bitcast.21), custom_call_target="tpu_custom_call" | custom-call | tf_op jit(solution)/shard_map/pallas_call | solution.py:843
  21.3 2.6 %all-to-all-start.1 = ((bf16[32,16,128]{2,1,0:T(8,128)(2,1)}), bf16[32,16,128]{2,1,0:T(8,128)(2,1)S(1)}, u32[]{:S(2)}, u32[]{:S(2)}) async-start(bf16[32,16,128]{2,1,0:T(8,128)(2,1)} %bitcast.6), calls=%async_computation.1 | async-start | bytes 262144 | tf_op jit(solution)/shard_map/all_to_all | solution.py:809
  24.0 8.3 %all-to-all-done.1.in_ref = bf16[32,16,128]{2,1,0:T(8,128)(2,1)S(1)} async-done(((bf16[32,16,128]{2,1,0:T(8,128)(2,1)}), bf16[32,16,128]{2,1,0:T(8,128)(2,1)S(1)}, u32[]{:S(2)}, u32[]{:S(2)}) %all-to-all-start.1) | async-done | bytes 131104 | tf_op jit(solution)/shard_map/all_to_all | solution.py:809
  32.3 3.7 %shard_map.218 = (bf16[512,128]{1,0:T(8,128)(2,1)}, f32[512,128]{1,0:T(8,128)}, bf16[8,4,16,128]{3,2,1,0:T(8,128)(2,1)}) custom-call(s32[2]{0:T(128)S(1)} %pad_add_fusion.here_ref, s32[128]{0:T(128)} %chain_ref.1, bf16[32,16,128]{2,1,0:T(8,128)(2,1)S(1)} %all-to-all-done.1.in_ref, bf16[512,128]{1,0:T(8,128)(2,1)} %bitcast.27, s32[1,128]{1,0:T(1,128)} %bitcast.31, ...), custom_call_target="tpu_custom_call" | custom-call | tf_op jit(solution)/shard_map/pallas_call | solution.py:847
  36.0 2.6 %all-to-all-start.2 = ((bf16[32,16,128]{2,1,0:T(8,128)(2,1)}), bf16[32,16,128]{2,1,0:T(8,128)(2,1)S(1)}, u32[]{:S(2)}, u32[]{:S(2)}) async-start(bf16[32,16,128]{2,1,0:T(8,128)(2,1)} %bitcast.13), calls=%async_computation.2 | async-start | bytes 262144 | tf_op jit(solution)/shard_map/all_to_all | solution.py:809
  38.6 0.6 broadcast_in_dim.26.gain_ref
  39.2 4.6 %shard_map.219 = (bf16[384,192]{1,0:T(8,128)(2,1)S(1)}, bf16[384,192]{1,0:T(8,128)(2,1)S(1)}, bf16[384,192]{1,0:T(8,128)(2,1)S(1)}, bf16[384,192]{1,0:T(8,128)(2...) custom-call(f32[3]{0:T(128)S(1)} %add_rsqrt_fusion.scale_ref, ...), custom_call_target="tpu_custom_call" | custom-call | tf_op jit(solution)/shard_map/pallas_call | solution.py:827
  43.8 3.2 %all-to-all-done.2 = bf16[32,16,128]{2,1,0:T(8,128)(2,1)S(1)} async-done(((bf16[32,16,128]{2,1,0:T(8,128)(2,1)}), bf16[32,16,128]{2,1,0:T(8,128)(2,1)S(1)}, u32[]{:S(2)}, u32[]{:S(2)}) %all-to-all-start.2) | async-done | bytes 131104 | tf_op jit(solution)/shard_map/all_to_all | solution.py:809
  46.9 4.7 %shard_map.220 = (bf16[8,4,16,128]{3,2,1,0:T(8,128)(2,1)}, bf16[384,192]{1,0:T(8,128)(2,1)}, bf16[4,384,192]{2,1,0:T(8,128)(2,1)}, bf16[3,32,1024]{2,1,0:T(8,128...) custom-call(s32[2]{0:T(128)S(1)} %pad_add_fusion.here_ref, ...), custom_call_target="tpu_custom_call" | custom-call | tf_op jit(solution)/shard_map/pallas_call | solution.py:881
  51.7 4.0 %shard_map.222 = (bf16[4,96,1024]{2,1,0:T(8,128)(2,1)S(1)}, bf16[4,96,1024]{2,1,0:T(8,128)(2,1)}) custom-call(s32[2]{0:T(128)S(1)} %pad_add_fusion.here_ref, bf16[768,384]{1,0:T(8,128)(2,1)} %get-tuple-element.59.hidden_t_ref, bf16[768,384]{1,0:T(8,128)(2,1)} %get-tuple-element.60.cot_t_ref, bf16[4,384,192]{2,1,0:T(8,128)(2,1)} %get-tuple-element.61.grads_ref, ...), custom_call_target="tpu_custom_call" | custom-call | tf_op jit(solution)/shard_map/pallas_call | solution.py:916
  55.7 2.8 %all-to-all-start.3 = ((bf16[32,16,128]{2,1,0:T(8,128)(2,1)}), bf16[32,16,128]{2,1,0:T(8,128)(2,1)S(1)}, u32[]{:S(2)}, u32[]{:S(2)}) async-start(bf16[32,16,128]{2,1,0:T(8,128)(2,1)} %bitcast.16), calls=%async_computation.3 | async-start | bytes 262144 | tf_op jit(solution)/shard_map/all_to_all | solution.py:809
  58.5 0.7 constant_dynamic-slice_fusion
  59.2 1.8 %collective-permute-start.3 = (bf16[96,768]{1,0:T(8,128)(2,1)}, bf16[96,768]{1,0:T(8,128)(2,1)S(1)}, u32[]{:S(2)}, u32[]{:S(2)}) collective-permute-start(bf16[96,768]{1,0:T(8,128)(2,1)} %constant_dynamic-slice_fusion), channel_id=1, source_target_pairs={{0,1},{1,2},{2,3},{3,0},{4,5},{5,6},{6,7},{7,4},{8,9},{9,10},{10,1... | collective-permute-start | bytes 442376 | tf_op jit(solution)/shard_map/ppermute | solution.py:812
  61.0 2.4 %collective-permute-start.4 = (bf16[96,768]{1,0:T(8,128)(2,1)}, bf16[96,768]{1,0:T(8,128)(2,1)}, u32[]{:S(2)}, u32[]{:S(2)}) collective-permute-start(bf16[96,768]{1,0:T(8,128)(2,1)} %constant_dynamic-slice_fusion), channel_id=1, source_target_pairs={{0,2},{1,3},{2,0},{3,1},{4,6},{5,7},{6,4},{7,5},{8,10},{9,11},{10,... | collective-permute-start | bytes 442376 | tf_op jit(solution)/shard_map/ppermute | solution.py:812
  63.4 1.4 %collective-permute-start.5 = (bf16[96,768]{1,0:T(8,128)(2,1)}, bf16[96,768]{1,0:T(8,128)(2,1)}, u32[]{:S(2)}, u32[]{:S(2)}) collective-permute-start(bf16[96,768]{1,0:T(8,128)(2,1)} %constant_dynamic-slice_fusion), channel_id=1, source_target_pairs={{0,3},{1,0},{2,1},{3,2},{4,7},{5,4},{6,5},{7,6},{8,11},{9,8},{10,9... | collective-permute-start | bytes 442376 | tf_op jit(solution)/shard_map/ppermute | solution.py:812
  64.9 4.2 %collective-permute-done.3.refs_4_ = bf16[96,768]{1,0:T(8,128)(2,1)S(1)} collective-permute-done((bf16[96,768]{1,0:T(8,128)(2,1)}, bf16[96,768]{1,0:T(8,128)(2,1)S(1)}, u32[]{:S(2)}, u32[]{:S(2)}) %collective-permute-start.3) | collective-permute-done | bytes 147488 | tf_op jit(solution)/shard_map/ppermute | solution.py:812
  69.1 4.2 %collective-permute-start = (bf16[3,32,1024]{2,1,0:T(8,128)(2,1)}, bf16[3,32,1024]{2,1,0:T(8,128)(2,1)}, u32[]{:S(2)}, u32[]{:S(2)}) collective-permute-start(bf16[3,32,1024]{2,1,0:T(8,128)(2,1)} %get-tuple-element.54), channel_id=1, source_target_pairs={{0,1},{1,2},{2,3},{3,0},{4,5},{5,6},{6,7},{7,4},{8,9},{9,10},{10,1... | collective-permute-start | bytes 589832 | tf_op jit(solution)/shard_map/ppermute | solution.py:812
  73.3 2.3 %shard_map.221 = (f32[512,128]{1,0:T(8,128)}, bf16[32,16,128]{2,1,0:T(8,128)(2,1)S(1)}) custom-call(bf16[8,4,16,128]{3,2,1,0:T(8,128)(2,1)S(1)} %bitcast.23, f32[512,128]{1,0:T(8,128)} %get-tuple-element.50.updated_ref, f32[1,128]{1,0:T(1,128)} %bitcast.35, bf16[16,128]{1,0:T(8,128)(2,1)} %bitcast.29), custom_call_target="tpu_custom_call" | custom-call | tf_op jit(solution)/shard_map/pallas_call | solution.py:943
  75.6 0.6 copy-done.4
  76.2 4.8 %all-to-all-start.4 = ((bf16[32,16,128]{2,1,0:T(8,128)(2,1)}), bf16[32,16,128]{2,1,0:T(8,128)(2,1)S(1)}, u32[]{:S(2)}, u32[]{:S(2)}) async-start(bf16[32,16,128]{2,1,0:T(8,128)(2,1)} %copy-done.4), calls=%async_computation.4 | async-start | bytes 262144 | tf_op jit(solution)/shard_map/all_to_all | solution.py:809
  81.6 2.7 %collective-permute-start.1 = (bf16[3,32,1024]{2,1,0:T(8,128)(2,1)}, bf16[3,32,1024]{2,1,0:T(8,128)(2,1)S(1)}, u32[]{:S(2)}, u32[]{:S(2)}) collective-permute-start(bf16[3,32,1024]{2,1,0:T(8,128)(2,1)} %get-tuple-element.55), channel_id=1, source_target_pairs={{0,2},{1,3},{2,0},{3,1},{4,6},{5,7},{6,4},{7,5},{8,10},{9,11},{10,... | collective-permute-start | bytes 589832 | tf_op jit(solution)/shard_map/ppermute | solution.py:812
  84.3 1.5 %collective-permute-start.2 = (bf16[3,32,1024]{2,1,0:T(8,128)(2,1)}, bf16[3,32,1024]{2,1,0:T(8,128)(2,1)S(1)}, u32[]{:S(2)}, u32[]{:S(2)}) collective-permute-start(bf16[3,32,1024]{2,1,0:T(8,128)(2,1)} %get-tuple-element.56), channel_id=1, source_target_pairs={{0,3},{1,0},{2,1},{3,2},{4,7},{5,4},{6,5},{7,6},{8,11},{9,8},{10,9... | collective-permute-start | bytes 589832 | tf_op jit(solution)/shard_map/ppermute | solution.py:812
  85.8 1.8 %shard_map.223 = (bf16[96,1024]{1,0:T(8,128)(2,1)}, bf16[96,1024]{1,0:T(8,128)(2,1)}, bf16[96,1024]{1,0:T(8,128)(2,1)}, bf16[96,1024]{1,0:T(8,128)(2,1)}) custom-call(s32[2]{0:T(128)S(1)} %pad_add_fusion.here_ref, bf16[4,96,1024]{2,1,0:T(8,128)(2,1)S(1)} %get-tuple-element.63.keep_ref, bf16[4,96,1024]{2,1,0:T(8,128)(2,1)S(1)} %collective-permute-done.9.got_ref), custom_call_target="tpu_custom_call" | custom-call | tf_op jit(solution)/shard_map/pallas_call | solution.py:925
  87.6 1.5 %collective-permute-start.10 = (bf16[96,1024]{1,0:T(8,128)(2,1)}, bf16[96,1024]{1,0:T(8,128)(2,1)S(1)}, u32[]{:S(2)}, u32[]{:S(2)}) collective-permute-start(bf16[96,1024]{1,0:T(8,128)(2,1)} %get-tuple-element.66), channel_id=1, source_target_pairs={{0,8},{4,12},{8,0},{12,4},{16,24},{20,28},{24,16},{28,20},{1,9},{5... | collective-permute-start | bytes 589832 | tf_op jit(solution)/shard_map/ppermute | solution.py:939
  89.1 1.5 %collective-permute-start.11 = (bf16[96,1024]{1,0:T(8,128)(2,1)}, bf16[96,1024]{1,0:T(8,128)(2,1)S(1)}, u32[]{:S(2)}, u32[]{:S(2)}) collective-permute-start(bf16[96,1024]{1,0:T(8,128)(2,1)} %get-tuple-element.67), channel_id=1, source_target_pairs={{0,16},{4,20},{8,24},{12,28},{16,0},{20,4},{24,8},{28,12},{1,17},{... | collective-permute-start | bytes 589832 | tf_op jit(solution)/shard_map/ppermute | solution.py:939
  90.5 0.6 collective-permute-start.12
  91.1 5.5 %collective-permute-done.1.refs_2_ = bf16[3,32,1024]{2,1,0:T(8,128)(2,1)S(1)} collective-permute-done((bf16[3,32,1024]{2,1,0:T(8,128)(2,1)}, bf16[3,32,1024]{2,1,0:T(8,128)(2,1)S(1)}, u32[]{:S(2)}, u32[]{:S(2)}) %collective-permute-start.1) | collective-permute-done | bytes 196640 | tf_op jit(solution)/shard_map/ppermute | solution.py:812
  96.6 3.0 %token_out.1 = (bf16[3,32,768]{2,1,0:T(8,128)(2,1)}, bf16[3,32,768]{2,1,0:T(8,128)(2,1)}) custom-call(s32[2]{0:T(128)S(1)} %pad_add_fusion.here_ref, f32[3]{0:T(128)S(1)} %add_rsqrt_fusion.scale_ref, bf16[3,128,768]{2,1,0:T(8,128)(2,1)S(1)} %copy-done, bf16[3,128,768]{2,1,0:T(8,128)(2,1)S(1)} %copy-done.1, f32[1,768]{1,0:T(1,128)S(1)} %copy-done.5, ...), custom_call_target="tpu_custom_call" | custom-call | tf_op jit(solution)/shard_map/token_out/pallas_call | solution.py:968
  99.6 0.6 convert_reduce_fusion
  100.2 1.8 %shard_map.224 = (f32[4,96,192]{2,1,0:T(8,128)}, f32[192,96]{1,0:T(8,128)}) custom-call(bf16[96,1024]{1,0:T(8,128)(2,1)} %get-tuple-element.65.refs_0_, bf16[96,1024]{1,0:T(8,128)(2,1)S(1)} %collective-permute-done.10.refs_1_, bf16[96,1024]{1,0:T(8,128)(2,1)S(1)} %collective-permute-done.11.refs_2_, bf16[96,1024]{1,0:T(8,128)(2,1)S(1)} %collective-permute-done.12.refs_3_), custom_call_target="tpu_custom_call" | custom-call | tf_op jit(solution)/shard_map/pallas_call | solution.py:956
  (34 shorter events, 0.7 us)
Async XLA Ops:
  0.6 37.9 %copy-start.6 = (f32[768]{0:T(1024)S(1)}, f32[768]{0:T(1024)}, u32[]{:S(2)}) copy-start(f32[768]{0:T(1024)} %param.30) | copy-start | bytes 9220
  0.6 38.5 %copy-start.7 = (s32[3]{0:T(128)S(1)}, s32[3]{0:T(128)}, u32[]{:S(2)}) copy-start(s32[3]{0:T(128)} %param.29) | copy-start | bytes 40
  21.3 11.0 %all-to-all-start.1 = ((bf16[32,16,128]{2,1,0:T(8,128)(2,1)}), bf16[32,16,128]{2,1,0:T(8,128)(2,1)S(1)}, u32[]{:S(2)}, u32[]{:S(2)}) async-start(bf16[32,16,128]{2,1,0:T(8,128)(2,1)} %bitcast.6), calls=%async_computation.1 | async-start | bytes 262144 | tf_op jit(solution)/shard_map/all_to_all | solution.py:809
  36.0 11.0 %all-to-all-start.2 = ((bf16[32,16,128]{2,1,0:T(8,128)(2,1)}), bf16[32,16,128]{2,1,0:T(8,128)(2,1)S(1)}, u32[]{:S(2)}, u32[]{:S(2)}) async-start(bf16[32,16,128]{2,1,0:T(8,128)(2,1)} %bitcast.13), calls=%async_computation.2 | async-start | bytes 262144 | tf_op jit(solution)/shard_map/all_to_all | solution.py:809
  51.7 6.8 %copy-start.2 = (bf16[192,768]{1,0:T(8,128)(2,1)S(1)}, bf16[192,768]{1,0:T(8,128)(2,1)}, u32[]{:S(2)}) copy-start(bf16[192,768]{1,0:T(8,128)(2,1)} %weight_ref.1) | copy-start | bytes 884740
  55.7 28.6 %collective-permute-start.9 = (bf16[4,96,1024]{2,1,0:T(8,128)(2,1)}, bf16[4,96,1024]{2,1,0:T(8,128)(2,1)S(1)}, u32[]{:S(2)}, u32[]{:S(2)}) collective-permute-start(bf16[4,96,1024]{2,1,0:T(8,128)(2,1)} %get-tuple-element.64), channel_id=1, source_target_pairs={{0,4},{4,0},{8,12},{12,8},{16,20},{20,16},{24,28},{28,24},{1,5},{5... | collective-permute-start | bytes 2359304 | tf_op jit(solution)/shard_map/ppermute | solution.py:924
  55.7 17.6 %all-to-all-start.3 = ((bf16[32,16,128]{2,1,0:T(8,128)(2,1)}), bf16[32,16,128]{2,1,0:T(8,128)(2,1)S(1)}, u32[]{:S(2)}, u32[]{:S(2)}) async-start(bf16[32,16,128]{2,1,0:T(8,128)(2,1)} %bitcast.16), calls=%async_computation.3 | async-start | bytes 262144 | tf_op jit(solution)/shard_map/all_to_all | solution.py:809
  59.2 37.4 %copy-start = (bf16[3,128,768]{2,1,0:T(8,128)(2,1)S(1)}, bf16[3,128,768]{2,1,0:T(8,128)(2,1)}, u32[]{:S(2)}) copy-start(bf16[3,128,768]{2,1,0:T(8,128)(2,1)} %tokens_ref.3) | copy-start | bytes 1769476
  59.2 37.4 %copy-start.1 = (bf16[3,128,768]{2,1,0:T(8,128)(2,1)S(1)}, bf16[3,128,768]{2,1,0:T(8,128)(2,1)}, u32[]{:S(2)}) copy-start(bf16[3,128,768]{2,1,0:T(8,128)(2,1)} %cot_ref.3) | copy-start | bytes 1769476
  59.2 37.4 %copy-start.3 = (bf16[3,32,1024]{2,1,0:T(8,128)(2,1)S(1)}, bf16[3,32,1024]{2,1,0:T(8,128)(2,1)}, u32[]{:S(2)}) copy-start(bf16[3,32,1024]{2,1,0:T(8,128)(2,1)} %get-tuple-element.53.refs_0_) | copy-start | bytes 589828
  59.2 37.4 %copy-start.5 = (f32[1,768]{1,0:T(1,128)S(1)}, f32[1,768]{1,0:T(1,128)}, u32[]{:S(2)}) copy-start(f32[1,768]{1,0:T(1,128)} %broadcast_in_dim.26.gain_ref) | copy-start | bytes 9220
  59.2 9.9 %collective-permute-start.3 = (bf16[96,768]{1,0:T(8,128)(2,1)}, bf16[96,768]{1,0:T(8,128)(2,1)S(1)}, u32[]{:S(2)}, u32[]{:S(2)}) collective-permute-start(bf16[96,768]{1,0:T(8,128)(2,1)} %constant_dynamic-slice_fusion), channel_id=1, source_target_pairs={{0,1},{1,2},{2,3},{3,0},{4,5},{5,6},{6,7},{7,4},{8,9},{9,10},{10,1... | collective-permute-start | bytes 442376 | tf_op jit(solution)/shard_map/ppermute | solution.py:812
  61.0 20.0 %collective-permute-start.4 = (bf16[96,768]{1,0:T(8,128)(2,1)}, bf16[96,768]{1,0:T(8,128)(2,1)}, u32[]{:S(2)}, u32[]{:S(2)}) collective-permute-start(bf16[96,768]{1,0:T(8,128)(2,1)} %constant_dynamic-slice_fusion), channel_id=1, source_target_pairs={{0,2},{1,3},{2,0},{3,1},{4,6},{5,7},{6,4},{7,5},{8,10},{9,11},{10,... | collective-permute-start | bytes 442376 | tf_op jit(solution)/shard_map/ppermute | solution.py:812
  63.4 17.9 %collective-permute-start.5 = (bf16[96,768]{1,0:T(8,128)(2,1)}, bf16[96,768]{1,0:T(8,128)(2,1)}, u32[]{:S(2)}, u32[]{:S(2)}) collective-permute-start(bf16[96,768]{1,0:T(8,128)(2,1)} %constant_dynamic-slice_fusion), channel_id=1, source_target_pairs={{0,3},{1,0},{2,1},{3,2},{4,7},{5,4},{6,5},{7,6},{8,11},{9,8},{10,9... | collective-permute-start | bytes 442376 | tf_op jit(solution)/shard_map/ppermute | solution.py:812
  69.1 12.5 %collective-permute-start.6 = (bf16[96,768]{1,0:T(8,128)(2,1)S(1)}, bf16[96,768]{1,0:T(8,128)(2,1)}, u32[]{:S(2)}, u32[]{:S(2)}) collective-permute-start(bf16[96,768]{1,0:T(8,128)(2,1)S(1)} %collective-permute-done.3.refs_4_), channel_id=1, source_target_pairs={{0,4},{4,0},{8,12},{12,8},{16,20},{20,16},{24,28},{28,24},{1,5},{5... | collective-permute-start | bytes 442376 | tf_op jit(solution)/shard_map/ppermute | solution.py:912
  69.1 21.4 %collective-permute-start = (bf16[3,32,1024]{2,1,0:T(8,128)(2,1)}, bf16[3,32,1024]{2,1,0:T(8,128)(2,1)}, u32[]{:S(2)}, u32[]{:S(2)}) collective-permute-start(bf16[3,32,1024]{2,1,0:T(8,128)(2,1)} %get-tuple-element.54), channel_id=1, source_target_pairs={{0,1},{1,2},{2,3},{3,0},{4,5},{5,6},{6,7},{7,4},{8,9},{9,10},{10,1... | collective-permute-start | bytes 589832 | tf_op jit(solution)/shard_map/ppermute | solution.py:812
  75.6 0.6 copy-start.4
  76.2 23.3 %all-to-all-start.4 = ((bf16[32,16,128]{2,1,0:T(8,128)(2,1)}), bf16[32,16,128]{2,1,0:T(8,128)(2,1)S(1)}, u32[]{:S(2)}, u32[]{:S(2)}) async-start(bf16[32,16,128]{2,1,0:T(8,128)(2,1)} %copy-done.4), calls=%async_computation.4 | async-start | bytes 262144 | tf_op jit(solution)/shard_map/all_to_all | solution.py:809
  81.0 6.6 %collective-permute-start.7 = (bf16[96,768]{1,0:T(8,128)(2,1)}, bf16[96,768]{1,0:T(8,128)(2,1)S(1)}, u32[]{:S(2)}, u32[]{:S(2)}) collective-permute-start(bf16[96,768]{1,0:T(8,128)(2,1)} %collective-permute-done.4.refs_5_), channel_id=1, source_target_pairs={{0,4},{4,0},{8,12},{12,8},{16,20},{20,16},{24,28},{28,24},{1,5},{5... | collective-permute-start | bytes 442376 | tf_op jit(solution)/shard_map/ppermute | solution.py:912
  81.4 7.7 %collective-permute-start.8 = (bf16[96,768]{1,0:T(8,128)(2,1)}, bf16[96,768]{1,0:T(8,128)(2,1)S(1)}, u32[]{:S(2)}, u32[]{:S(2)}) collective-permute-start(bf16[96,768]{1,0:T(8,128)(2,1)} %collective-permute-done.5.refs_6_), channel_id=1, source_target_pairs={{0,4},{4,0},{8,12},{12,8},{16,20},{20,16},{24,28},{28,24},{1,5},{5... | collective-permute-start | bytes 442376 | tf_op jit(solution)/shard_map/ppermute | solution.py:912
  81.6 14.9 %collective-permute-start.1 = (bf16[3,32,1024]{2,1,0:T(8,128)(2,1)}, bf16[3,32,1024]{2,1,0:T(8,128)(2,1)S(1)}, u32[]{:S(2)}, u32[]{:S(2)}) collective-permute-start(bf16[3,32,1024]{2,1,0:T(8,128)(2,1)} %get-tuple-element.55), channel_id=1, source_target_pairs={{0,2},{1,3},{2,0},{3,1},{4,6},{5,7},{6,4},{7,5},{8,10},{9,11},{10,... | collective-permute-start | bytes 589832 | tf_op jit(solution)/shard_map/ppermute | solution.py:812
  84.3 12.3 %collective-permute-start.2 = (bf16[3,32,1024]{2,1,0:T(8,128)(2,1)}, bf16[3,32,1024]{2,1,0:T(8,128)(2,1)S(1)}, u32[]{:S(2)}, u32[]{:S(2)}) collective-permute-start(bf16[3,32,1024]{2,1,0:T(8,128)(2,1)} %get-tuple-element.56), channel_id=1, source_target_pairs={{0,3},{1,0},{2,1},{3,2},{4,7},{5,4},{6,5},{7,6},{8,11},{9,8},{10,9... | collective-permute-start | bytes 589832 | tf_op jit(solution)/shard_map/ppermute | solution.py:812
  87.6 12.6 %collective-permute-start.10 = (bf16[96,1024]{1,0:T(8,128)(2,1)}, bf16[96,1024]{1,0:T(8,128)(2,1)S(1)}, u32[]{:S(2)}, u32[]{:S(2)}) collective-permute-start(bf16[96,1024]{1,0:T(8,128)(2,1)} %get-tuple-element.66), channel_id=1, source_target_pairs={{0,8},{4,12},{8,0},{12,4},{16,24},{20,28},{24,16},{28,20},{1,9},{5... | collective-permute-start | bytes 589832 | tf_op jit(solution)/shard_map/ppermute | solution.py:939
  89.1 11.2 %collective-permute-start.11 = (bf16[96,1024]{1,0:T(8,128)(2,1)}, bf16[96,1024]{1,0:T(8,128)(2,1)S(1)}, u32[]{:S(2)}, u32[]{:S(2)}) collective-permute-start(bf16[96,1024]{1,0:T(8,128)(2,1)} %get-tuple-element.67), channel_id=1, source_target_pairs={{0,16},{4,20},{8,24},{12,28},{16,0},{20,4},{24,8},{28,12},{1,17},{... | collective-permute-start | bytes 589832 | tf_op jit(solution)/shard_map/ppermute | solution.py:939
  90.5 9.7 %collective-permute-start.12 = (bf16[96,1024]{1,0:T(8,128)(2,1)}, bf16[96,1024]{1,0:T(8,128)(2,1)S(1)}, u32[]{:S(2)}, u32[]{:S(2)}) collective-permute-start(bf16[96,1024]{1,0:T(8,128)(2,1)} %get-tuple-element.68), channel_id=1, source_target_pairs={{0,24},{4,28},{8,16},{12,20},{16,8},{20,12},{24,0},{28,4},{1,25},{... | collective-permute-start | bytes 589832 | tf_op jit(solution)/shard_map/ppermute | solution.py:939

commit v2 on v1

--- a/solution.py
+++ b/solution.py
@@ -347,16 +347,25 @@
         )
 
 
+def pair_gate_kernel(
+    pair_ref, gain_ref, gate_ref, out_gain_ref, out_weight_ref, out_ref, *, devices
+):
+    pairs, channels = pair_ref.shape
+    pair_in = (normalize(pair_ref[...].astype(jnp.float32)) * gain_ref[...]).astype(jnp.bfloat16)
+    out_ref[:pairs] = jax.nn.sigmoid(dot_nn(pair_in, gate_ref[...]))
+    order = channel_order(channels, devices)
+    gain_t = jnp.sum(jnp.where(order, out_gain_ref[...], 0.0), axis=1, keepdims=True)
+    order_b = order.astype(jnp.float32).astype(jnp.bfloat16)
+    out_ref[pairs:] = dot_nn(order_b, out_weight_ref[...]) * gain_t
+
+
 def pair_out_kernel(
     here_ref,
     chain_ref,
     in_ref,
     pair_ref,
     chain_row_ref,
-    in_gain_ref,
     gate_ref,
-    out_gain_ref,
-    out_weight_ref,
     bias_gain_ref,
     bias_weight_ref,
     chain_bias_ref,
@@ -400,14 +409,9 @@
             )
         )
     normed_t = jnp.concatenate(blocks, axis=1)
-    order = channel_order(channels, devices)
-    gain_t = jnp.sum(jnp.where(order, out_gain_ref[...], 0.0), axis=1, keepdims=True)
-    order_b = order.astype(jnp.float32).astype(jnp.bfloat16)
-    weight = dot_nn(order_b, out_weight_ref[...]).astype(jnp.bfloat16)
-    update = dot_tn((normed_t * gain_t).astype(jnp.bfloat16), weight)
-    pair = pair_ref[...].astype(jnp.float32)
-    pair_in = (normalize(pair) * in_gain_ref[...]).astype(jnp.bfloat16)
-    updated = pair + jax.nn.sigmoid(dot_nn(pair_in, gate_ref[...])) * update
+    pairs = pair_ref.shape[0]
+    update = dot_tn(normed_t.astype(jnp.bfloat16), gate_ref[pairs:].astype(jnp.bfloat16))
+    updated = pair_ref[...].astype(jnp.float32) + gate_ref[:pairs] * update
     updated_ref[...] = updated
     next_ref[...] = updated.astype(jnp.bfloat16)
     bias_in = (normalize(updated) * bias_gain_ref[...]).astype(jnp.bfloat16)
@@ -844,6 +848,9 @@
         triangle_kernel, 8, whole((stripes, cols, rows, LANES), bf16), 0, 1, width=width
     )(sides.reshape(stripes, cols, 2, rows, LANES))
     triangle = exchange(triangle.reshape(devices, rows, LANES), all_axes)
+    pair_gate = call(
+        pair_gate_kernel, 8, pltpu.VMEM((pairs + channels, LANES), f32), 0, 5, devices=devices
+    )(*map(far, (pair_flat, tri_in_gain[None], tri_gate, tri_out_gain[None], tri_out)))
     pair_next, updated, bias_tile = call(
         pair_out_kernel,
         8,
@@ -853,7 +860,7 @@
             whole((stripes, cols, rows, LANES), bf16),
         ),
         2,
-        10,
+        7,
         [pltpu.VMEM((devices * rows, LANES), f32)],
         width=width,
     )(
@@ -865,15 +872,10 @@
             (
                 pair_flat,
                 chain_id[None],
-                tri_in_gain[None],
-                tri_gate,
-                tri_out_gain[None],
-                tri_out,
-                bias_gain[None],
-                bias_weight_t,
-                chain_bias[None],
             ),
         ),
+        near(pair_gate),
+        *map(far, (bias_gain[None], bias_weight_t, chain_bias[None])),
     )
     head_bias = exchange(bias_tile.reshape(devices, rows, LANES), all_axes)
     share = length // cols
@@ -962,7 +964,7 @@
         ),
         0,
         chips,
-    )(far(wires[0]), *map(near, wires[1:]))
+    )(near(wires[0]), *map(near, wires[1:]))
     mine = pl.BlockSpec((copies, share, hidden_width), lambda i, here: (0, here[1], 0))
     fixed = lambda shape: pl.BlockSpec(shape, lambda i, here: (0,) * len(shape))
     denoised, token_grad = pl.pallas_call(

time: 104 us -> 102 us (0.981)
  waiting for transfers between devices: 21.2 us -> 19.9 us
    all_to_all x4, waiting for transfers between devices: 11.5 us -> 10.2 us  [exchange(): return lax.all_to_all(values, axes, 0, 0, tiled=True)]
    pallas_call x0 -> x1, Pallas kernels: none -> 1.3 us  [shards(): call(pair_gate_kernel, 8, pltpu.VMEM((pairs + channels, LANES), f32), 0,...]
  transfers between devices with their start and end apart: 17 -> 17, of which waited for: 4 -> 4; matrix products, arithmetic and copies ran while one was open for 2% -> 2% of each run, Pallas kernels for 12% -> 13%
where the time goes in v2:
time: 102 us; the launch traced here: 100 us
  starting transfers between devices  30.8 us (30%)
  Pallas kernels  28.7 us (28%)
  waiting for transfers between devices  19.9 us (20%)
  blocking collectives  17.4 us (17%)
  local copies, waits for them, and re-layouts  1.94 us (2%)
    all_to_all x1, blocking collectives, exchange(): return lax.all_to_all(values, axes, 0, 0, tiled=True)  17.4 us
    ppermute x6, starting transfers between devices, shift(): lax.ppermute(values, 'col', [(i, (i + k) % cols) for i in range(cols)])  14 us
    all_to_all x4, starting transfers between devices, exchange(): return lax.all_to_all(values, axes, 0, 0, tiled=True)  12.7 us
    all_to_all x4, waiting for transfers between devices, exchange(): return lax.all_to_all(values, axes, 0, 0, tiled=True)  10.2 us
    ppermute x6, waiting for transfers between devices, shift(): lax.ppermute(values, 'col', [(i, (i + k) % cols) for i in range(cols)])  9.71 us
    pallas_call x1, Pallas kernels, shards(): call(attention_kernel, 20, (pltpu.HBM((stripes, cols, rows, LANES), bf16)...  4.7 us
    pallas_call x1, Pallas kernels, shards(): call(token_in_kernel, 16, (*[pltpu.VMEM((tall, inner), bf16)] * 4, *[pltp...  4.59 us
    pallas_call x1, Pallas kernels, shards(): call(weight_in_kernel, 16, (pltpu.VMEM((chips, block, 8 * LANES), bf16),)...  4.03 us
  transfers between devices with their start and end apart: 17, of which 4 were waited for; matrix products, arithmetic and copies ran while one was open for 2% of the time, Pallas kernels for 13%

profile of v2, /device:TPU:0, one launch (start us, length us, event | category | flops | bytes accessed | tf_op | source)
XLA Modules:
  0.0 100.2 jit_solution(12119735844880937292)
XLA Ops:
  0.6 2.0 %shard_map.216 = bf16[32,2,16,128]{3,2,1,0:T(8,128)(2,1)S(1)} custom-call(bf16[512,128]{1,0:T(8,128)(2,1)} %bitcast.26, s32[16,32]{1,0:T(8,128)} %mask_ref.1, f32[1,128]{1,0:T(1,128)} %bitcast.32, bf16[128,512]{1,0:T(8,128)(2,1)} %proj_ref.1), custom_call_target="tpu_custom_call" | custom-call | tf_op jit(solution)/shard_map/pallas_call | solution.py:818
  2.6 17.4 %all_to_all.25 = bf16[32,32,128]{2,1,0:T(8,128)(2,1)S(1)} all-to-all(bf16[32,32,128]{2,1,0:T(8,128)(2,1)S(1)} %bitcast.20), channel_id=1, replica_groups=mesh['group'=2,'row'=4,'col'=4] {'group','row','col'}, dimensions={0} | all-to-all | bytes 524288 | tf_op jit(solution)/shard_map/all_to_all | solution.py:813
  20.0 1.2 %shard_map.217 = bf16[8,4,16,128]{3,2,1,0:T(8,128)(2,1)} custom-call(bf16[8,4,2,16,128]{4,3,2,1,0:T(8,128)(2,1)S(1)} %bitcast.21), custom_call_target="tpu_custom_call" | custom-call | tf_op jit(solution)/shard_map/pallas_call | solution.py:847
  21.3 2.6 %all-to-all-start.1 = ((bf16[32,16,128]{2,1,0:T(8,128)(2,1)}), bf16[32,16,128]{2,1,0:T(8,128)(2,1)S(1)}, u32[]{:S(2)}, u32[]{:S(2)}) async-start(bf16[32,16,128]{2,1,0:T(8,128)(2,1)} %bitcast.6), calls=%async_computation.1 | async-start | bytes 262144 | tf_op jit(solution)/shard_map/all_to_all | solution.py:813
  23.9 1.3 %shard_map.218.gate_ref = f32[640,128]{1,0:T(8,128)S(1)} custom-call(bf16[512,128]{1,0:T(8,128)(2,1)} %bitcast.27, f32[1,128]{1,0:T(1,128)} %bitcast.33, bf16[128,128]{1,0:T(8,128)(2,1)} %gate_ref.1, f32[1,128]{1,0:T(1,128)} %bitcast.37, bf16[128,128]{1,0:T(8,128)(2,1)} %out_weight_ref.2), custom_call_target="tpu_custom_call" | custom-call | tf_op jit(solution)/shard_map/pallas_call | solution.py:851
  25.3 7.0 %all-to-all-done.1.in_ref = bf16[32,16,128]{2,1,0:T(8,128)(2,1)S(1)} async-done(((bf16[32,16,128]{2,1,0:T(8,128)(2,1)}), bf16[32,16,128]{2,1,0:T(8,128)(2,1)S(1)}, u32[]{:S(2)}, u32[]{:S(2)}) %all-to-all-start.1) | async-done | bytes 131104 | tf_op jit(solution)/shard_map/all_to_all | solution.py:813
  32.3 2.8 %shard_map.219 = (bf16[512,128]{1,0:T(8,128)(2,1)}, f32[512,128]{1,0:T(8,128)}, bf16[8,4,16,128]{3,2,1,0:T(8,128)(2,1)}) custom-call(s32[2]{0:T(128)S(1)} %pad_add_fusion.here_ref, s32[128]{0:T(128)} %chain_ref.1, bf16[32,16,128]{2,1,0:T(8,128)(2,1)S(1)} %all-to-all-done.1.in_ref, bf16[512,128]{1,0:T(8,128)(2,1)} %bitcast.28, s32[1,128]{1,0:T(1,128)} %bitcast.36, ...), custom_call_target="tpu_custom_call" | custom-call | tf_op jit(solution)/shard_map/pallas_call | solution.py:854
  35.1 2.6 %all-to-all-start.2 = ((bf16[32,16,128]{2,1,0:T(8,128)(2,1)}), bf16[32,16,128]{2,1,0:T(8,128)(2,1)S(1)}, u32[]{:S(2)}, u32[]{:S(2)}) async-start(bf16[32,16,128]{2,1,0:T(8,128)(2,1)} %bitcast.13), calls=%async_computation.2 | async-start | bytes 262144 | tf_op jit(solution)/shard_map/all_to_all | solution.py:813
  37.7 0.6 broadcast_in_dim.26.gain_ref
  38.3 4.6 %shard_map.220 = (bf16[384,192]{1,0:T(8,128)(2,1)S(1)}, bf16[384,192]{1,0:T(8,128)(2,1)S(1)}, bf16[384,192]{1,0:T(8,128)(2,1)S(1)}, bf16[384,192]{1,0:T(8,128)(2...) custom-call(f32[3]{0:T(128)S(1)} %add_rsqrt_fusion.scale_ref, ...), custom_call_target="tpu_custom_call" | custom-call | tf_op jit(solution)/shard_map/pallas_call | solution.py:831
  42.8 3.2 %all-to-all-done.2 = bf16[32,16,128]{2,1,0:T(8,128)(2,1)S(1)} async-done(((bf16[32,16,128]{2,1,0:T(8,128)(2,1)}), bf16[32,16,128]{2,1,0:T(8,128)(2,1)S(1)}, u32[]{:S(2)}, u32[]{:S(2)}) %all-to-all-start.2) | async-done | bytes 131104 | tf_op jit(solution)/shard_map/all_to_all | solution.py:813
  46.0 4.7 %shard_map.221 = (bf16[8,4,16,128]{3,2,1,0:T(8,128)(2,1)}, bf16[384,192]{1,0:T(8,128)(2,1)}, bf16[4,384,192]{2,1,0:T(8,128)(2,1)}, bf16[3,32,1024]{2,1,0:T(8,128...) custom-call(s32[2]{0:T(128)S(1)} %pad_add_fusion.here_ref, ...), custom_call_target="tpu_custom_call" | custom-call | tf_op jit(solution)/shard_map/pallas_call | solution.py:883
  50.7 4.0 %shard_map.223 = (bf16[4,96,1024]{2,1,0:T(8,128)(2,1)S(1)}, bf16[4,96,1024]{2,1,0:T(8,128)(2,1)}) custom-call(s32[2]{0:T(128)S(1)} %pad_add_fusion.here_ref, bf16[768,384]{1,0:T(8,128)(2,1)} %get-tuple-element.59.hidden_t_ref, bf16[768,384]{1,0:T(8,128)(2,1)} %get-tuple-element.60.cot_t_ref, bf16[4,384,192]{2,1,0:T(8,128)(2,1)} %get-tuple-element.61.grads_ref, ...), custom_call_target="tpu_custom_call" | custom-call | tf_op jit(solution)/shard_map/pallas_call | solution.py:918
  54.8 2.8 %all-to-all-start.3 = ((bf16[32,16,128]{2,1,0:T(8,128)(2,1)}), bf16[32,16,128]{2,1,0:T(8,128)(2,1)S(1)}, u32[]{:S(2)}, u32[]{:S(2)}) async-start(bf16[32,16,128]{2,1,0:T(8,128)(2,1)} %bitcast.16), calls=%async_computation.3 | async-start | bytes 262144 | tf_op jit(solution)/shard_map/all_to_all | solution.py:813
  57.6 0.7 constant_dynamic-slice_fusion
  58.3 1.8 %collective-permute-start.3 = (bf16[96,768]{1,0:T(8,128)(2,1)}, bf16[96,768]{1,0:T(8,128)(2,1)S(1)}, u32[]{:S(2)}, u32[]{:S(2)}) collective-permute-start(bf16[96,768]{1,0:T(8,128)(2,1)} %constant_dynamic-slice_fusion), channel_id=1, source_target_pairs={{0,1},{1,2},{2,3},{3,0},{4,5},{5,6},{6,7},{7,4},{8,9},{9,10},{10,1... | collective-permute-start | bytes 442376 | tf_op jit(solution)/shard_map/ppermute | solution.py:816
  60.1 2.4 %collective-permute-start.4 = (bf16[96,768]{1,0:T(8,128)(2,1)}, bf16[96,768]{1,0:T(8,128)(2,1)}, u32[]{:S(2)}, u32[]{:S(2)}) collective-permute-start(bf16[96,768]{1,0:T(8,128)(2,1)} %constant_dynamic-slice_fusion), channel_id=1, source_target_pairs={{0,2},{1,3},{2,0},{3,1},{4,6},{5,7},{6,4},{7,5},{8,10},{9,11},{10,... | collective-permute-start | bytes 442376 | tf_op jit(solution)/shard_map/ppermute | solution.py:816
  62.5 1.4 %collective-permute-start.5 = (bf16[96,768]{1,0:T(8,128)(2,1)}, bf16[96,768]{1,0:T(8,128)(2,1)}, u32[]{:S(2)}, u32[]{:S(2)}) collective-permute-start(bf16[96,768]{1,0:T(8,128)(2,1)} %constant_dynamic-slice_fusion), channel_id=1, source_target_pairs={{0,3},{1,0},{2,1},{3,2},{4,7},{5,4},{6,5},{7,6},{8,11},{9,8},{10,9... | collective-permute-start | bytes 442376 | tf_op jit(solution)/shard_map/ppermute | solution.py:816
  63.9 4.2 %collective-permute-done.3.refs_4_ = bf16[96,768]{1,0:T(8,128)(2,1)S(1)} collective-permute-done((bf16[96,768]{1,0:T(8,128)(2,1)}, bf16[96,768]{1,0:T(8,128)(2,1)S(1)}, u32[]{:S(2)}, u32[]{:S(2)}) %collective-permute-start.3) | collective-permute-done | bytes 147488 | tf_op jit(solution)/shard_map/ppermute | solution.py:816
  68.1 4.2 %collective-permute-start = (bf16[3,32,1024]{2,1,0:T(8,128)(2,1)}, bf16[3,32,1024]{2,1,0:T(8,128)(2,1)}, u32[]{:S(2)}, u32[]{:S(2)}) collective-permute-start(bf16[3,32,1024]{2,1,0:T(8,128)(2,1)} %get-tuple-element.54), channel_id=1, source_target_pairs={{0,1},{1,2},{2,3},{3,0},{4,5},{5,6},{6,7},{7,4},{8,9},{9,10},{10,1... | collective-permute-start | bytes 589832 | tf_op jit(solution)/shard_map/ppermute | solution.py:816
  72.3 2.3 %shard_map.222 = (f32[512,128]{1,0:T(8,128)}, bf16[32,16,128]{2,1,0:T(8,128)(2,1)S(1)}) custom-call(bf16[8,4,16,128]{3,2,1,0:T(8,128)(2,1)S(1)} %bitcast.23, f32[512,128]{1,0:T(8,128)} %get-tuple-element.50.updated_ref, f32[1,128]{1,0:T(1,128)} %bitcast.35, bf16[16,128]{1,0:T(8,128)(2,1)} %bitcast.30), custom_call_target="tpu_custom_call" | custom-call | tf_op jit(solution)/shard_map/pallas_call | solution.py:945
  74.7 0.6 copy-done.5
  75.3 4.8 %all-to-all-start.4 = ((bf16[32,16,128]{2,1,0:T(8,128)(2,1)}), bf16[32,16,128]{2,1,0:T(8,128)(2,1)S(1)}, u32[]{:S(2)}, u32[]{:S(2)}) async-start(bf16[32,16,128]{2,1,0:T(8,128)(2,1)} %copy-done.5), calls=%async_computation.4 | async-start | bytes 262144 | tf_op jit(solution)/shard_map/all_to_all | solution.py:813
  80.7 2.7 %collective-permute-start.1 = (bf16[3,32,1024]{2,1,0:T(8,128)(2,1)}, bf16[3,32,1024]{2,1,0:T(8,128)(2,1)S(1)}, u32[]{:S(2)}, u32[]{:S(2)}) collective-permute-start(bf16[3,32,1024]{2,1,0:T(8,128)(2,1)} %get-tuple-element.55), channel_id=1, source_target_pairs={{0,2},{1,3},{2,0},{3,1},{4,6},{5,7},{6,4},{7,5},{8,10},{9,11},{10,... | collective-permute-start | bytes 589832 | tf_op jit(solution)/shard_map/ppermute | solution.py:816
  83.3 1.5 %collective-permute-start.2 = (bf16[3,32,1024]{2,1,0:T(8,128)(2,1)}, bf16[3,32,1024]{2,1,0:T(8,128)(2,1)S(1)}, u32[]{:S(2)}, u32[]{:S(2)}) collective-permute-start(bf16[3,32,1024]{2,1,0:T(8,128)(2,1)} %get-tuple-element.56), channel_id=1, source_target_pairs={{0,3},{1,0},{2,1},{3,2},{4,7},{5,4},{6,5},{7,6},{8,11},{9,8},{10,9... | collective-permute-start | bytes 589832 | tf_op jit(solution)/shard_map/ppermute | solution.py:816
  84.8 1.8 %shard_map.224 = (bf16[96,1024]{1,0:T(8,128)(2,1)}, bf16[96,1024]{1,0:T(8,128)(2,1)}, bf16[96,1024]{1,0:T(8,128)(2,1)}, bf16[96,1024]{1,0:T(8,128)(2,1)}) custom-call(s32[2]{0:T(128)S(1)} %pad_add_fusion.here_ref, bf16[4,96,1024]{2,1,0:T(8,128)(2,1)S(1)} %get-tuple-element.63.keep_ref, bf16[4,96,1024]{2,1,0:T(8,128)(2,1)S(1)} %collective-permute-done.9.got_ref), custom_call_target="tpu_custom_call" | custom-call | tf_op jit(solution)/shard_map/pallas_call | solution.py:927
  86.6 1.5 %collective-permute-start.10 = (bf16[96,1024]{1,0:T(8,128)(2,1)}, bf16[96,1024]{1,0:T(8,128)(2,1)S(1)}, u32[]{:S(2)}, u32[]{:S(2)}) collective-permute-start(bf16[96,1024]{1,0:T(8,128)(2,1)} %get-tuple-element.66), channel_id=1, source_target_pairs={{0,8},{4,12},{8,0},{12,4},{16,24},{20,28},{24,16},{28,20},{1,9},{5... | collective-permute-start | bytes 589832 | tf_op jit(solution)/shard_map/ppermute | solution.py:941
  88.1 1.5 %collective-permute-start.11 = (bf16[96,1024]{1,0:T(8,128)(2,1)}, bf16[96,1024]{1,0:T(8,128)(2,1)S(1)}, u32[]{:S(2)}, u32[]{:S(2)}) collective-permute-start(bf16[96,1024]{1,0:T(8,128)(2,1)} %get-tuple-element.67), channel_id=1, source_target_pairs={{0,16},{4,20},{8,24},{12,28},{16,0},{20,4},{24,8},{28,12},{1,17},{... | collective-permute-start | bytes 589832 | tf_op jit(solution)/shard_map/ppermute | solution.py:941
  90.1 5.5 %collective-permute-done.1.refs_2_ = bf16[3,32,1024]{2,1,0:T(8,128)(2,1)S(1)} collective-permute-done((bf16[3,32,1024]{2,1,0:T(8,128)(2,1)}, bf16[3,32,1024]{2,1,0:T(8,128)(2,1)S(1)}, u32[]{:S(2)}, u32[]{:S(2)}) %collective-permute-start.1) | collective-permute-done | bytes 196640 | tf_op jit(solution)/shard_map/ppermute | solution.py:816
  95.7 3.0 %token_out.1 = (bf16[3,32,768]{2,1,0:T(8,128)(2,1)}, bf16[3,32,768]{2,1,0:T(8,128)(2,1)}) custom-call(s32[2]{0:T(128)S(1)} %pad_add_fusion.here_ref, f32[3]{0:T(128)S(1)} %add_rsqrt_fusion.scale_ref, bf16[3,128,768]{2,1,0:T(8,128)(2,1)S(1)} %copy-done, bf16[3,128,768]{2,1,0:T(8,128)(2,1)S(1)} %copy-done.1, f32[1,768]{1,0:T(1,128)S(1)} %copy-done.6, ...), custom_call_target="tpu_custom_call" | custom-call | tf_op jit(solution)/shard_map/token_out/pallas_call | solution.py:970
  98.6 0.6 convert_reduce_fusion
  99.3 0.9 shard_map.225
  (37 shorter events, 1.3 us)
Async XLA Ops:
  2.6 35.0 %copy-start.7 = (f32[768]{0:T(1024)S(1)}, f32[768]{0:T(1024)}, u32[]{:S(2)}) copy-start(f32[768]{0:T(1024)} %param.30) | copy-start | bytes 9220
  2.6 35.6 %copy-start.8 = (s32[3]{0:T(128)S(1)}, s32[3]{0:T(128)}, u32[]{:S(2)}) copy-start(s32[3]{0:T(128)} %param.29) | copy-start | bytes 40
  21.3 11.0 %all-to-all-start.1 = ((bf16[32,16,128]{2,1,0:T(8,128)(2,1)}), bf16[32,16,128]{2,1,0:T(8,128)(2,1)S(1)}, u32[]{:S(2)}, u32[]{:S(2)}) async-start(bf16[32,16,128]{2,1,0:T(8,128)(2,1)} %bitcast.6), calls=%async_computation.1 | async-start | bytes 262144 | tf_op jit(solution)/shard_map/all_to_all | solution.py:813
  35.1 11.0 %all-to-all-start.2 = ((bf16[32,16,128]{2,1,0:T(8,128)(2,1)}), bf16[32,16,128]{2,1,0:T(8,128)(2,1)S(1)}, u32[]{:S(2)}, u32[]{:S(2)}) async-start(bf16[32,16,128]{2,1,0:T(8,128)(2,1)} %bitcast.13), calls=%async_computation.2 | async-start | bytes 262144 | tf_op jit(solution)/shard_map/all_to_all | solution.py:813
  50.7 6.8 %copy-start.2 = (bf16[192,768]{1,0:T(8,128)(2,1)S(1)}, bf16[192,768]{1,0:T(8,128)(2,1)}, u32[]{:S(2)}) copy-start(bf16[192,768]{1,0:T(8,128)(2,1)} %weight_ref.1) | copy-start | bytes 884740
  54.8 28.6 %collective-permute-start.9 = (bf16[4,96,1024]{2,1,0:T(8,128)(2,1)}, bf16[4,96,1024]{2,1,0:T(8,128)(2,1)S(1)}, u32[]{:S(2)}, u32[]{:S(2)}) collective-permute-start(bf16[4,96,1024]{2,1,0:T(8,128)(2,1)} %get-tuple-element.64), channel_id=1, source_target_pairs={{0,4},{4,0},{8,12},{12,8},{16,20},{20,16},{24,28},{28,24},{1,5},{5... | collective-permute-start | bytes 2359304 | tf_op jit(solution)/shard_map/ppermute | solution.py:926
  54.8 17.5 %all-to-all-start.3 = ((bf16[32,16,128]{2,1,0:T(8,128)(2,1)}), bf16[32,16,128]{2,1,0:T(8,128)(2,1)S(1)}, u32[]{:S(2)}, u32[]{:S(2)}) async-start(bf16[32,16,128]{2,1,0:T(8,128)(2,1)} %bitcast.16), calls=%async_computation.3 | async-start | bytes 262144 | tf_op jit(solution)/shard_map/all_to_all | solution.py:813
  58.2 37.4 %copy-start = (bf16[3,128,768]{2,1,0:T(8,128)(2,1)S(1)}, bf16[3,128,768]{2,1,0:T(8,128)(2,1)}, u32[]{:S(2)}) copy-start(bf16[3,128,768]{2,1,0:T(8,128)(2,1)} %tokens_ref.3) | copy-start | bytes 1769476
  58.2 37.4 %copy-start.1 = (bf16[3,128,768]{2,1,0:T(8,128)(2,1)S(1)}, bf16[3,128,768]{2,1,0:T(8,128)(2,1)}, u32[]{:S(2)}) copy-start(bf16[3,128,768]{2,1,0:T(8,128)(2,1)} %cot_ref.3) | copy-start | bytes 1769476
  58.2 37.4 %copy-start.3 = (bf16[3,32,1024]{2,1,0:T(8,128)(2,1)S(1)}, bf16[3,32,1024]{2,1,0:T(8,128)(2,1)}, u32[]{:S(2)}) copy-start(bf16[3,32,1024]{2,1,0:T(8,128)(2,1)} %get-tuple-element.53.refs_0_) | copy-start | bytes 589828
  58.2 37.4 %copy-start.6 = (f32[1,768]{1,0:T(1,128)S(1)}, f32[1,768]{1,0:T(1,128)}, u32[]{:S(2)}) copy-start(f32[1,768]{1,0:T(1,128)} %broadcast_in_dim.26.gain_ref) | copy-start | bytes 9220
  58.3 9.9 %collective-permute-start.3 = (bf16[96,768]{1,0:T(8,128)(2,1)}, bf16[96,768]{1,0:T(8,128)(2,1)S(1)}, u32[]{:S(2)}, u32[]{:S(2)}) collective-permute-start(bf16[96,768]{1,0:T(8,128)(2,1)} %constant_dynamic-slice_fusion), channel_id=1, source_target_pairs={{0,1},{1,2},{2,3},{3,0},{4,5},{5,6},{6,7},{7,4},{8,9},{9,10},{10,1... | collective-permute-start | bytes 442376 | tf_op jit(solution)/shard_map/ppermute | solution.py:816
  60.1 20.0 %collective-permute-start.4 = (bf16[96,768]{1,0:T(8,128)(2,1)}, bf16[96,768]{1,0:T(8,128)(2,1)}, u32[]{:S(2)}, u32[]{:S(2)}) collective-permute-start(bf16[96,768]{1,0:T(8,128)(2,1)} %constant_dynamic-slice_fusion), channel_id=1, source_target_pairs={{0,2},{1,3},{2,0},{3,1},{4,6},{5,7},{6,4},{7,5},{8,10},{9,11},{10,... | collective-permute-start | bytes 442376 | tf_op jit(solution)/shard_map/ppermute | solution.py:816
  62.5 17.9 %collective-permute-start.5 = (bf16[96,768]{1,0:T(8,128)(2,1)}, bf16[96,768]{1,0:T(8,128)(2,1)}, u32[]{:S(2)}, u32[]{:S(2)}) collective-permute-start(bf16[96,768]{1,0:T(8,128)(2,1)} %constant_dynamic-slice_fusion), channel_id=1, source_target_pairs={{0,3},{1,0},{2,1},{3,2},{4,7},{5,4},{6,5},{7,6},{8,11},{9,8},{10,9... | collective-permute-start | bytes 442376 | tf_op jit(solution)/shard_map/ppermute | solution.py:816
  68.1 12.6 %collective-permute-start.6 = (bf16[96,768]{1,0:T(8,128)(2,1)S(1)}, bf16[96,768]{1,0:T(8,128)(2,1)}, u32[]{:S(2)}, u32[]{:S(2)}) collective-permute-start(bf16[96,768]{1,0:T(8,128)(2,1)S(1)} %collective-permute-done.3.refs_4_), channel_id=1, source_target_pairs={{0,4},{4,0},{8,12},{12,8},{16,20},{20,16},{24,28},{28,24},{1,5},{5... | collective-permute-start | bytes 442376 | tf_op jit(solution)/shard_map/ppermute | solution.py:914
  68.1 21.4 %collective-permute-start = (bf16[3,32,1024]{2,1,0:T(8,128)(2,1)}, bf16[3,32,1024]{2,1,0:T(8,128)(2,1)}, u32[]{:S(2)}, u32[]{:S(2)}) collective-permute-start(bf16[3,32,1024]{2,1,0:T(8,128)(2,1)} %get-tuple-element.54), channel_id=1, source_target_pairs={{0,1},{1,2},{2,3},{3,0},{4,5},{5,6},{6,7},{7,4},{8,9},{9,10},{10,1... | collective-permute-start | bytes 589832 | tf_op jit(solution)/shard_map/ppermute | solution.py:816
  74.7 0.6 copy-start.5
  75.3 23.3 %all-to-all-start.4 = ((bf16[32,16,128]{2,1,0:T(8,128)(2,1)}), bf16[32,16,128]{2,1,0:T(8,128)(2,1)S(1)}, u32[]{:S(2)}, u32[]{:S(2)}) async-start(bf16[32,16,128]{2,1,0:T(8,128)(2,1)} %copy-done.5), calls=%async_computation.4 | async-start | bytes 262144 | tf_op jit(solution)/shard_map/all_to_all | solution.py:813
  80.1 6.5 %collective-permute-start.7 = (bf16[96,768]{1,0:T(8,128)(2,1)}, bf16[96,768]{1,0:T(8,128)(2,1)S(1)}, u32[]{:S(2)}, u32[]{:S(2)}) collective-permute-start(bf16[96,768]{1,0:T(8,128)(2,1)} %collective-permute-done.4.refs_5_), channel_id=1, source_target_pairs={{0,4},{4,0},{8,12},{12,8},{16,20},{20,16},{24,28},{28,24},{1,5},{5... | collective-permute-start | bytes 442376 | tf_op jit(solution)/shard_map/ppermute | solution.py:914
  80.4 7.7 %collective-permute-start.8 = (bf16[96,768]{1,0:T(8,128)(2,1)}, bf16[96,768]{1,0:T(8,128)(2,1)S(1)}, u32[]{:S(2)}, u32[]{:S(2)}) collective-permute-start(bf16[96,768]{1,0:T(8,128)(2,1)} %collective-permute-done.5.refs_6_), channel_id=1, source_target_pairs={{0,4},{4,0},{8,12},{12,8},{16,20},{20,16},{24,28},{28,24},{1,5},{5... | collective-permute-start | bytes 442376 | tf_op jit(solution)/shard_map/ppermute | solution.py:914
  80.7 14.9 %collective-permute-start.1 = (bf16[3,32,1024]{2,1,0:T(8,128)(2,1)}, bf16[3,32,1024]{2,1,0:T(8,128)(2,1)S(1)}, u32[]{:S(2)}, u32[]{:S(2)}) collective-permute-start(bf16[3,32,1024]{2,1,0:T(8,128)(2,1)} %get-tuple-element.55), channel_id=1, source_target_pairs={{0,2},{1,3},{2,0},{3,1},{4,6},{5,7},{6,4},{7,5},{8,10},{9,11},{10,... | collective-permute-start | bytes 589832 | tf_op jit(solution)/shard_map/ppermute | solution.py:816
  83.3 12.3 %collective-permute-start.2 = (bf16[3,32,1024]{2,1,0:T(8,128)(2,1)}, bf16[3,32,1024]{2,1,0:T(8,128)(2,1)S(1)}, u32[]{:S(2)}, u32[]{:S(2)}) collective-permute-start(bf16[3,32,1024]{2,1,0:T(8,128)(2,1)} %get-tuple-element.56), channel_id=1, source_target_pairs={{0,3},{1,0},{2,1},{3,2},{4,7},{5,4},{6,5},{7,6},{8,11},{9,8},{10,9... | collective-permute-start | bytes 589832 | tf_op jit(solution)/shard_map/ppermute | solution.py:816
  86.6 12.7 %collective-permute-start.10 = (bf16[96,1024]{1,0:T(8,128)(2,1)}, bf16[96,1024]{1,0:T(8,128)(2,1)S(1)}, u32[]{:S(2)}, u32[]{:S(2)}) collective-permute-start(bf16[96,1024]{1,0:T(8,128)(2,1)} %get-tuple-element.66), channel_id=1, source_target_pairs={{0,8},{4,12},{8,0},{12,4},{16,24},{20,28},{24,16},{28,20},{1,9},{5... | collective-permute-start | bytes 589832 | tf_op jit(solution)/shard_map/ppermute | solution.py:941
  88.1 11.2 %collective-permute-start.11 = (bf16[96,1024]{1,0:T(8,128)(2,1)}, bf16[96,1024]{1,0:T(8,128)(2,1)S(1)}, u32[]{:S(2)}, u32[]{:S(2)}) collective-permute-start(bf16[96,1024]{1,0:T(8,128)(2,1)} %get-tuple-element.67), channel_id=1, source_target_pairs={{0,16},{4,20},{8,24},{12,28},{16,0},{20,4},{24,8},{28,12},{1,17},{... | collective-permute-start | bytes 589832 | tf_op jit(solution)/shard_map/ppermute | solution.py:941
  89.6 9.7 %collective-permute-start.12 = (bf16[96,1024]{1,0:T(8,128)(2,1)}, bf16[96,1024]{1,0:T(8,128)(2,1)S(1)}, u32[]{:S(2)}, u32[]{:S(2)}) collective-permute-start(bf16[96,1024]{1,0:T(8,128)(2,1)} %get-tuple-element.68), channel_id=1, source_target_pairs={{0,24},{4,28},{8,16},{12,20},{16,8},{20,12},{24,0},{28,4},{1,25},{... | collective-permute-start | bytes 589832 | tf_op jit(solution)/shard_map/ppermute | solution.py:941
  95.6 3.6 %copy-start.4 = (bf16[96,1024]{1,0:T(8,128)(2,1)S(1)}, bf16[96,1024]{1,0:T(8,128)(2,1)}, u32[]{:S(2)}) copy-start(bf16[96,1024]{1,0:T(8,128)(2,1)} %get-tuple-element.65.refs_0_) | copy-start | bytes 589828
